TPU v7x, 32 devices: a whole 2x2x4 slice. The times are simulated.
32 devices in a mesh: member: 2 (over x), lat: 16 (over z, y, core).
Axes of the slice: x: 2, y: 2, z: 4, core: 2. Of those that a mesh axis runs over, the one named last changes fastest.
Arguments:
- field: bfloat16 [192, 1440, 256], P(('member', 'lat')), parts along dimension 0, may hold values from -3000 to 3000
- gain: float32 [256], replicated, may hold values from 0.1 to 1.9
- slot_wave: int32 [96], replicated, may hold values from 0 to 96, as said below
- legendre: bfloat16 [96, 96, 96], P('lat'), may hold values from -0.625 to 0.625
- mixing: bfloat16 [96, 2, 256, 256], P('lat'), may hold values from -0.25 to 0.25
Outputs:
- result: bfloat16 [192, 1440, 256], P(('member', 'lat')), parts along dimension 0
There are 2 independent parts, one for each index of `member`. A program takes and returns all parts, laid end to end along the dimension named above; an argument that names none is the same for every part. Nothing has to cross between parts.
Inputs may be any that keep to these rules, and one draw needn't show every extreme that they name: `slot_wave`: each wavenumber 0 to 95 stands in exactly one slot and every other slot holds 96; slots 2k and 2k+1 of one lat index hold wavenumbers adding up to (4k+2)16 - 1 where both are below 96.
All inputs are finite; a program needn't handle non-finite values.
Results may differ from a plain program's by a relative error of at most 0.0085.
Values may be sent and summed in bfloat16 or wider, within the bound.
A program may use at most 64 MiB of HBM per device.

v0:
```python
import functools
import math

import jax
import jax.numpy as jnp
import numpy as np
from jax import lax
from jax.experimental import pallas as pl
from jax.experimental.pallas import tpu as pltpu
from jax.sharding import PartitionSpec as P

MESH = pl.DeviceIdType.MESH
F32 = jnp.float32
BF16 = jnp.bfloat16


def wave_table(degs, width):
    pad = -(-(degs + 1) // 128) * 128
    waves = np.arange(degs + 1)[:, None]
    phase = (waves * np.arange(width)[None, :] % width) * (2.0 * np.pi / width)
    table = np.zeros((2, pad, width), np.float32)
    table[0, : degs + 1] = np.cos(phase)
    table[1, : degs + 1] = -np.sin(phase)
    return table.reshape(2 * pad, width).astype(BF16), pad


def dot(a, b):
    return jnp.dot(a, b, preferred_element_type=F32)


def partner(me, step, count):
    if count & (count - 1):
        return lax.rem(me + step, count)
    out = 0
    for bit in range(count.bit_length() - 1):
        size = 2**bit
        mine = lax.rem(me // size, 2)
        flip = lax.rem(step // size, 2)
        out = out + size * (mine + flip - 2 * mine * flip)
    return out


def exchange_kernel(
    count,
    pad,
    field_ref, wave_hbm, wave_row_hbm, gain_hbm, table_hbm, tsum_hbm, legendre_hbm, mixing_hbm,
    ret_ref, target_ref, field_v,
    wave_ref, wave_row_ref, gain_ref, table_ref, tsum_row_ref, legendre_ref, mix_v,
    select, raw, spec, send, recv, back_send, stat_src, stat_recv, lbig,
    field_sem, load_sem, stat_sems, fwd_sems, back_sems,
):
    me = lax.axis_index("lat")
    lat_dev, width, chans = field_v.shape
    slot_dev, degs, nlat = legendre_ref.shape
    groups, lat_pairs = slot_dev // 2, lat_dev // 2
    rows = count * 8
    others = count - 1
    inv_root = 1.0 / math.sqrt(width)
    total_cells = float(lat_dev * count * width)

    barrier = pltpu.get_barrier_semaphore()

    def greet(step, carry):
        pl.semaphore_signal(barrier, inc=1, device_id={"lat": partner(me, step, count)}, device_id_type=MESH)
        return carry

    def load_of(index, source, target):
        load = pltpu.make_async_copy(source, target, load_sem.at[index])
        load.start()
        return load

    row_load = load_of(0, wave_row_hbm, wave_row_ref)
    table_load = load_of(1, table_hbm, table_ref)
    tsum_load = load_of(2, tsum_hbm, tsum_row_ref)
    loads = []
    for a in range(lat_dev):
        load = pltpu.make_async_copy(field_ref.at[a], field_v.at[a], field_sem.at[a])
        load.start()
        loads.append(load)
    late = [
        load_of(3, wave_hbm, wave_ref),
        load_of(4, legendre_hbm, legendre_ref),
        load_of(5, gain_hbm, gain_ref),
        load_of(6, mixing_hbm, mix_v),
    ]
    lax.fori_loop(1, count, greet, 0)

    slots = count * slot_dev
    row_load.wait()
    wave_row = wave_row_ref[...].astype(F32)
    columns = lax.broadcasted_iota(jnp.int32, (rows, 4 * pad), 1).astype(F32)
    row = lax.broadcasted_iota(jnp.int32, (rows, 1), 0)
    slot_lane = lax.broadcasted_iota(jnp.int32, (rows, slots), 1)
    for k in range(groups):
        slot_of = row // 8 * slot_dev + 2 * k + row % 4 // 2
        wave_of = jnp.sum(jnp.where(slot_lane == slot_of, wave_row, 0.0), axis=1, keepdims=True)
        target = wave_of + ((row % 8 // 4 * 2 + row % 2) * pad).astype(F32)
        select[k] = jnp.where(columns == target, 1.0, 0.0).astype(BF16)

    tsum_load.wait()
    part_a = lax.broadcasted_iota(jnp.int32, (2 * pad, 2 * pad), 0)
    part_b = lax.broadcasted_iota(jnp.int32, (2 * pad, 2 * pad), 1)
    tsum_col = jnp.sum(jnp.where(part_a == part_b, tsum_row_ref[...], 0.0), axis=1, keepdims=True)
    table_load.wait()
    squares = jnp.zeros((8, chans), F32)
    sums = jnp.zeros((1, chans), F32)
    for a in range(lat_dev):
        loads[a].wait()
        raw[a] = dot(table_ref[...], field_v[a])
        sums = sums + raw[a, 0:1, :]
        values = field_v[a].astype(F32)
        squares = squares + jnp.sum((values * values).reshape(width // 8, 8, chans), axis=0)
    square = jnp.sum(squares, axis=0, keepdims=True)
    own = jnp.concatenate([sums, square], axis=0)
    stat_src[...] = own
    stat_recv[pl.ds(me, 1)] = own[None]
    local_mean = sums / float(lat_dev * width)

    pl.semaphore_wait(barrier, others)

    def start_stat(step, carry):
        to = partner(me, count - step, count)
        pltpu.make_async_remote_copy(
            src_ref=stat_src, dst_ref=stat_recv.at[me], send_sem=stat_sems.at[0], recv_sem=stat_sems.at[1],
            device_id={"lat": to}, device_id_type=MESH,
        ).start()
        return carry

    lax.fori_loop(1, count, start_stat, 0)

    def start_group(k, source, target, sems):
        def body(step, carry):
            to = partner(me, count - step, count)
            pltpu.make_async_remote_copy(
                src_ref=source.at[k, to], dst_ref=target.at[k, me], send_sem=sems.at[0, k], recv_sem=sems.at[1, k],
                device_id={"lat": to}, device_id_type=MESH,
            ).start()
            return carry

        lax.fori_loop(1, count, body, 0)

    def wait_bytes(ref, sem):
        pltpu.make_async_copy(ref, ref, sem).wait()

    half = 2 * pad
    for p in range(lat_pairs):
        for parity in range(2):
            spec[p, parity * half : (parity + 1) * half, :] = (
                raw[2 * p + parity] - tsum_col * local_mean
            ).astype(BF16)
    for k in range(groups):
        for p in range(lat_pairs):
            picked = dot(select[k], spec[p])
            send[k, :, p] = picked.reshape(count, 8, chans).astype(BF16)
        recv[k, pl.ds(me, 1)] = send[k, pl.ds(me, 1)]
        start_group(k, send, recv, fwd_sems)

    for load in late:
        load.wait()
    slot_a = lax.broadcasted_iota(jnp.int32, (slots, slots), 0)
    slot_b = lax.broadcasted_iota(jnp.int32, (slots, slots), 1)
    wave_col = jnp.sum(jnp.where(slot_a == slot_b, wave_row, 0.0), axis=1, keepdims=True)
    lane = lax.broadcasted_iota(jnp.int32, (1, rows), 1)
    slot_line = lax.broadcasted_iota(jnp.int32, (slots, rows), 0)
    for k in range(groups):
        slot_of = lane // 8 * slot_dev + 2 * k + lane % 4 // 2
        wave_of = jnp.sum(jnp.where(slot_line == slot_of, wave_col, 0.0), axis=0, keepdims=True)
        target_ref[:, k * rows : (k + 1) * rows] = wave_of + ((lane % 8 // 4 * 2 + lane % 2) * pad).astype(F32)

    col = lax.broadcasted_iota(jnp.int32, (nlat, 4 * nlat), 1)
    lat_row = lax.broadcasted_iota(jnp.int32, (nlat, 4 * nlat), 0)
    degree = lax.broadcasted_iota(jnp.int32, (degs, nlat), 0)
    for k in range(groups):
        for jj in range(2):
            slot = 2 * k + jj
            wave = wave_ref[me * slot_dev + slot]
            kept = jnp.where(degree >= wave, legendre_ref[slot].astype(F32), 0.0).astype(BF16)
            for r in range(2):
                q = 2 * jj + r
                spread = jnp.where(col == 4 * lat_row + q, 1.0, 0.0).astype(BF16)
                lbig[k, q * degs : (q + 1) * degs, :] = dot(kept, spread).astype(BF16)

    wait_bytes(stat_recv.at[pl.ds(0, others)], stat_sems.at[1])
    stats = stat_recv[...]
    total = jnp.sum(stats, axis=0)
    mean = total[0:1] / total_cells
    var = total[1:2] / total_cells - mean * mean
    scale = gain_ref[...] / jnp.sqrt(var + 1e-05)
    shift = (stats[:, 0, :] / float(lat_dev * width) - mean).astype(BF16)
    owner = lax.broadcasted_iota(jnp.int32, (4 * nlat, count), 1)
    lat_of = lax.broadcasted_iota(jnp.int32, (4 * nlat, count), 0)
    owned = jnp.where((lat_of >= owner * (4 * lat_dev)) & (lat_of < (owner + 1) * (4 * lat_dev)), 1.0, 0.0).astype(BF16)
    shift_lat = dot(owned, shift).astype(BF16)
    mode_scale = scale * inv_root
    lanes = lax.broadcasted_iota(jnp.int32, (1, 2 * pad), 1)

    def normalize(a):
        field_v[a] = ((field_v[a].astype(F32) - mean) * scale).astype(BF16)

    for k in range(groups):
        if k > 0:
            for a in range((k - 1) * lat_dev // groups, k * lat_dev // groups):
                normalize(a)
        wait_bytes(recv.at[k, pl.ds(0, others)], fwd_sems.at[1, k])
        arrived = recv[k].astype(F32).reshape(count * lat_pairs * 8, chans).astype(BF16)
        coef = dot(lbig[k], arrived)
        offset = dot(lbig[k], shift_lat)
        mixed = []
        for jj in range(2):
            slot = 2 * k + jj
            wave = wave_ref[me * slot_dev + slot]
            parts = []
            for r in range(2):
                q = slice((2 * jj + r) * degs, (2 * jj + r + 1) * degs)
                tsum = jnp.sum(jnp.where(lanes == wave + r * pad, tsum_row_ref[...], 0.0), axis=1, keepdims=True)
                parts.append(((coef[q] + tsum * offset[q]) * mode_scale).astype(BF16))
            both = jnp.concatenate(parts, axis=0)
            by_real = dot(both, mix_v[slot, 0])
            by_imag = dot(both, mix_v[slot, 1])
            weight = jnp.where(wave == 0, 1.0, 2.0) * (math.sqrt(nlat / degs) * inv_root)
            mixed.append(((by_real[:degs] - by_imag[degs:]) * weight).astype(BF16))
            mixed.append(((by_imag[:degs] + by_real[degs:]) * weight).astype(BF16))
        mixed = jnp.concatenate(mixed, axis=0)
        back = lax.dot_general(lbig[k], mixed, (((0,), (0,)), ((), ())), preferred_element_type=F32)
        back_send[k] = back.reshape(count, lat_pairs, 8, chans).astype(BF16)
        ret_ref[k, pl.ds(me, 1)] = back_send[k, pl.ds(me, 1)]
        start_group(k, back_send, ret_ref, back_sems)

    for a in range((groups - 1) * lat_dev // groups, lat_dev):
        normalize(a)
    wait_bytes(stat_recv.at[pl.ds(0, others)], stat_sems.at[0])
    for k in range(groups):
        wait_bytes(send.at[k, pl.ds(0, others)], fwd_sems.at[0, k])
    for k in range(groups):
        wait_bytes(ret_ref.at[k, pl.ds(0, others)], back_sems.at[1, k])
        wait_bytes(back_send.at[k, pl.ds(0, others)], back_sems.at[0, k])


def inverse_kernel(pad, ret_ref, target_ref, table_ref, normed_ref, out_ref):
    groups, count, lat_pairs, _, chans = ret_ref.shape
    a = pl.program_id(0)
    pair, parity = a // 2, lax.rem(a, 2)
    rows = groups * count * 8
    line = (lax.broadcasted_iota(jnp.int32, (2 * pad, rows), 0) + parity * (2 * pad)).astype(F32)
    place = jnp.where(line == target_ref[...], 1.0, 0.0).astype(BF16)
    block = ret_ref[:, :, pl.ds(pair, 1)].astype(F32).reshape(rows, chans).astype(BF16)
    filtered = dot(table_ref[...], dot(place, block).astype(BF16))
    out_ref[0] = (normed_ref[a].astype(F32) + filtered).astype(BF16)


def per_device(field, gain, slot_wave, legendre, mixing):
    count = lax.axis_size("lat")
    lat_dev, width, chans = field.shape
    slot_dev, degs, nlat = legendre.shape
    groups, lat_pairs = slot_dev // 2, lat_dev // 2
    table, pad = wave_table(degs, width)
    tsum = table.astype(np.float64).sum(axis=1).astype(np.float32)
    rows = count * 8
    vmem = pl.BlockSpec(memory_space=pltpu.VMEM)
    hbm = pl.BlockSpec(memory_space=pltpu.HBM)
    dma = pltpu.SemaphoreType.DMA
    half_limit = 30 * 2**20
    block = (groups, count, lat_pairs, 8, chans)
    ret, target, normed = pl.pallas_call(
        functools.partial(exchange_kernel, count, pad),
        out_shape=(
            jax.ShapeDtypeStruct(block, BF16),
            jax.ShapeDtypeStruct((1, groups * rows), F32),
            jax.ShapeDtypeStruct(field.shape, BF16),
        ),
        in_specs=[hbm] * 8,
        out_specs=(vmem, vmem, vmem),
        scratch_shapes=[
            pltpu.SMEM(slot_wave.shape, jnp.int32),
            pltpu.VMEM((1,) + slot_wave.shape, jnp.int32),
            pltpu.VMEM((1, chans), F32),
            pltpu.VMEM(table.shape, BF16),
            pltpu.VMEM((1, 2 * pad), F32),
            pltpu.VMEM(legendre.shape, BF16),
            pltpu.VMEM(mixing.shape, BF16),
            pltpu.VMEM((groups, rows, 4 * pad), BF16),
            pltpu.VMEM((lat_dev, 2 * pad, chans), F32),
            pltpu.VMEM((lat_pairs, 4 * pad, chans), BF16),
            pltpu.VMEM(block, BF16),
            pltpu.VMEM(block, BF16),
            pltpu.VMEM(block, BF16),
            pltpu.VMEM((2, chans), F32),
            pltpu.VMEM((count, 2, chans), F32),
            pltpu.VMEM((groups, 4 * degs, 4 * nlat), BF16),
            dma((lat_dev,)),
            dma((7,)),
            dma((2,)),
            dma((2, groups)),
            dma((2, groups)),
        ],
        compiler_params=pltpu.CompilerParams(
            collective_id=0, has_side_effects=True, vmem_limit_bytes=half_limit if count <= 16 else 2 * half_limit
        ),
        name="exchange",
    )(*(pltpu.with_memory_space_constraint(x, pltpu.HBM) for x in (
        field, slot_wave, slot_wave.reshape(1, -1), gain.reshape(1, chans), jnp.asarray(table),
        jnp.asarray(tsum.reshape(1, -1)), legendre, mixing,
    )))
    return pl.pallas_call(
        functools.partial(inverse_kernel, pad),
        grid=(lat_dev,),
        out_shape=jax.ShapeDtypeStruct(field.shape, BF16),
        in_specs=[vmem, vmem, vmem, vmem],
        out_specs=pl.BlockSpec((1, width, chans), lambda a: (a, 0, 0)),
        compiler_params=pltpu.CompilerParams(vmem_limit_bytes=half_limit),
        name="inverse",
    )(ret, target, jnp.asarray(table.T.copy()), normed)


def solution(mesh):
    return jax.shard_map(
        per_device,
        mesh=mesh,
        in_specs=(
            P(("member", "lat"), None, None),
            P(),
            P(),
            P("lat", None, None),
            P("lat", None, None, None),
        ),
        out_specs=P(("member", "lat"), None, None),
        check_vma=False,
    )
```

profile of v0, /device:TPU:0, one launch (start us, length us, event | category | flops | bytes accessed | tf_op | source)
XLA Modules:
  0.0 42.4 jit_solution(17879899608382737369)
XLA Ops:
  0.0 0.0 copy-start
  0.0 37.0 %exchange.1 = (bf16[3,16,3,8,256]{4,3,2,1,0:T(8,128)(2,1)S(1)}, f32[1,384]{1,0:T(1,128)S(1)}, bf16[6,1440,256]{2,1,0:T(8,128)(2,1)S(1)}) custom-call(bf16[6,1440,256]{2,1,0:T(8,128)(2,1)} %field_ref.1, s32[96]{0:T(128)} %wave_hbm.1, s32[1,96]{1,0:T(1,128)} %bitcast.2, f32[1,256]{1,0:T(1,128)} %bitcast.3, bf16[256,1440]{1,0:T(8,128)(2,1)} %constant.6.clone.table_hbm, ...), custom_call_target="tpu_custom_call" | custom-call | tf_op jit(solution)/shard_map/exchange/pallas_call | solution.py:264
  37.1 0.0 copy-done
  37.1 5.3 %inverse.1 = bf16[6,1440,256]{2,1,0:T(8,128)(2,1)} custom-call(bf16[3,16,3,8,256]{4,3,2,1,0:T(8,128)(2,1)S(1)} %get-tuple-element.8.ret_ref, f32[1,384]{1,0:T(1,128)S(1)} %get-tuple-element.9.target_ref, bf16[1440,256]{1,0:T(8,128)(2,1)S(1)} %copy-done, bf16[6,1440,256]{2,1,0:T(8,128)(2,1)S(1)} %get-tuple-element.10.normed_ref), custom_call_target="tpu_custom_call" | custom-call | tf_op jit(solution)/shard_map/inverse/pallas_call | solution.py:304
Async XLA Ops:
  0.0 37.1 %copy-start = (bf16[1440,256]{1,0:T(8,128)(2,1)S(1)}, bf16[1440,256]{1,0:T(8,128)(2,1)}, u32[]{:S(2)}) copy-start(bf16[1440,256]{1,0:T(8,128)(2,1)} %constant.8.clone.table_ref) | copy-start | bytes 2211844
where the time goes:
time: 42.5 us; the launch traced here: 42.4 us
  Pallas kernels  42.4 us (100%)
    pallas_call x1, Pallas kernels, per_device(): pl.pallas_call(functools.partial(exchange_kernel, count, pad), out_shape=...  37 us
    pallas_call x1, Pallas kernels, per_device(): pl.pallas_call(functools.partial(inverse_kernel, pad), grid=(lat_dev,), o...  5.33 us

commit v1 on v0

v1 whole, which is shorter than its diff:
```python
import functools
import math

import jax
import jax.numpy as jnp
import numpy as np
from jax import lax
from jax.experimental import pallas as pl
from jax.experimental.pallas import tpu as pltpu
from jax.sharding import PartitionSpec as P

MESH = pl.DeviceIdType.MESH
F32 = jnp.float32
BF16 = jnp.bfloat16


def wave_table(degs, width):
    pad = -(-(degs + 1) // 128) * 128
    waves = np.arange(degs + 1)[:, None]
    phase = (waves * np.arange(width)[None, :] % width) * (2.0 * np.pi / width)
    table = np.zeros((2, pad, width), np.float32)
    table[0, : degs + 1] = np.cos(phase)
    table[1, : degs + 1] = -np.sin(phase)
    return table.reshape(2 * pad, width).astype(BF16), pad


def dot(a, b):
    return jnp.dot(a, b, preferred_element_type=F32)


def partner(me, step, count):
    if count & (count - 1):
        return lax.rem(me + step, count)
    out = 0
    for bit in range(count.bit_length() - 1):
        size = 2**bit
        mine = lax.rem(me // size, 2)
        flip = lax.rem(step // size, 2)
        out = out + size * (mine + flip - 2 * mine * flip)
    return out


def packed_rows(k, count, slot_dev, degs):
    if count % 2 or count * slot_dev != degs:
        return degs + degs
    return 2 * degs + 1 - (4 * k + 2) * count


def exchange_kernel(
    count,
    pad,
    relay,
    kept_rows,
    field_ref, wave_hbm, wave_row_hbm, gain_hbm, table_hbm, tsum_hbm, legendre_hbm, mixing_hbm, back_table_hbm,
    field_v, placed_ref,
    wave_ref, wave_row_ref, gain_ref, table_ref, tsum_row_ref, legendre_ref, mix_v, back_table,
    select, raw, spec, send, recv, back_send, ret, stat_src, stat_recv, lbig, place,
    near_recv, near_back, part_send, part_recv, mixed_send, mixed_recv, pack_send, pack_recv, pack_own, pack_mate,
    field_sem, load_sem, stat_sems, fwd_sems, back_sems, last_sems, pack_sems, part_sems, mixed_sems, near_sems,
):
    me = lax.axis_index("lat")
    lat_dev, width, chans = field_v.shape
    slot_dev, degs, nlat = legendre_ref.shape
    groups, lat_pairs = slot_dev // 2, lat_dev // 2
    rows = count * 8
    others = count - 1
    inv_root = 1.0 / math.sqrt(width)
    total_cells = float(lat_dev * count * width)
    near = count // 2
    side = me // near
    spot = me - side * near
    mate = lax.rem(me + near, count)
    direct = [k for k in range(groups) if k != relay]
    final = direct[-1]
    order = ([relay] if relay is not None else []) + direct
    slot_at = {k: i for i, k in enumerate(direct)}

    barrier = pltpu.get_barrier_semaphore()

    def greet(step, carry):
        pl.semaphore_signal(barrier, inc=1, device_id={"lat": partner(me, step, count)}, device_id_type=MESH)
        return carry

    def load_of(index, source, target):
        load = pltpu.make_async_copy(source, target, load_sem.at[index])
        load.start()
        return load

    row_load = load_of(0, wave_row_hbm, wave_row_ref)
    table_load = load_of(1, table_hbm, table_ref)
    tsum_load = load_of(2, tsum_hbm, tsum_row_ref)
    loads = []
    for a in range(lat_dev):
        load = pltpu.make_async_copy(field_ref.at[a], field_v.at[a], field_sem.at[a])
        load.start()
        loads.append(load)
    late = [
        load_of(3, wave_hbm, wave_ref),
        load_of(4, legendre_hbm, legendre_ref),
        load_of(5, gain_hbm, gain_ref),
        load_of(6, mixing_hbm, mix_v),
        load_of(7, back_table_hbm, back_table),
    ]
    lax.fori_loop(1, count, greet, 0)

    def copy_to(to, source, target, sems):
        pltpu.make_async_remote_copy(
            src_ref=source, dst_ref=target, send_sem=sems.at[0], recv_sem=sems.at[1],
            device_id={"lat": to}, device_id_type=MESH,
        ).start()

    def to_all(source, target, sems):
        def body(step, carry):
            to = partner(me, count - step, count)
            copy_to(to, source(to), target, sems)
            return carry

        lax.fori_loop(1, count, body, 0)

    def to_near(source, target, sems):
        def body(step, carry):
            there = partner(spot, near - step, near)
            copy_to(side * near + there, source(there), target, sems)
            return carry

        lax.fori_loop(1, near, body, 0)

    def wait_bytes(ref, sem):
        pltpu.make_async_copy(ref, ref, sem).wait()

    def merged(block):
        return block.astype(F32).reshape(-1, chans).astype(BF16)

    slots = count * slot_dev
    row_load.wait()
    wave_row = wave_row_ref[...].astype(F32)
    columns = lax.broadcasted_iota(jnp.int32, (rows, 4 * pad), 1).astype(F32)
    row = lax.broadcasted_iota(jnp.int32, (rows, 1), 0)
    slot_lane = lax.broadcasted_iota(jnp.int32, (rows, slots), 1)
    for k in range(groups):
        slot_of = row // 8 * slot_dev + 2 * k + row % 4 // 2
        wave_of = jnp.sum(jnp.where(slot_lane == slot_of, wave_row, 0.0), axis=1, keepdims=True)
        target = wave_of + ((row % 8 // 4 * 2 + row % 2) * pad).astype(F32)
        select[k] = jnp.where(columns == target, 1.0, 0.0).astype(BF16)

    tsum_load.wait()
    part_a = lax.broadcasted_iota(jnp.int32, (2 * pad, 2 * pad), 0)
    part_b = lax.broadcasted_iota(jnp.int32, (2 * pad, 2 * pad), 1)
    tsum_col = jnp.sum(jnp.where(part_a == part_b, tsum_row_ref[...], 0.0), axis=1, keepdims=True)
    table_load.wait()
    sums = jnp.zeros((1, chans), F32)
    for a in range(lat_dev):
        loads[a].wait()
        raw[a] = dot(table_ref[...], field_v[a])
        sums = sums + raw[a, 0:1, :]
    local_mean = sums / float(lat_dev * width)

    half = 2 * pad
    for p in range(lat_pairs):
        for parity in range(2):
            spec[p, parity * half : (parity + 1) * half, :] = (
                raw[2 * p + parity] - tsum_col * local_mean
            ).astype(BF16)

    def pick(k):
        for p in range(lat_pairs):
            picked = dot(select[k], spec[p])
            send[k, :, p] = picked.reshape(count, 8, chans).astype(BF16)

    def start_forward(k):
        i = slot_at[k]
        recv[i, pl.ds(me, 1)] = send[k, pl.ds(me, 1)]
        to_all(lambda to: send.at[k, to], recv.at[i, me], fwd_sems.at[k])

    for load in late:
        load.wait()

    if relay is not None:
        first, second = 2 * relay, 2 * relay + 1
        high = pack_own.shape[0]
        tall, hold = pack_send.shape
        degree_at = lax.broadcasted_iota(jnp.int32, (tall, degs), 1)
        degree_row = lax.broadcasted_iota(jnp.int32, (tall, degs), 0)
        lead = degs - wave_ref[me * slot_dev + first]
        from_first = (degree_row < lead) & (degree_at == degs - 1 - degree_row)
        from_second = (degree_row >= lead) & (degree_row < kept_rows) & (degree_at == degree_row + (degs - kept_rows))
        packed = (
            dot(jnp.where(from_first, 1.0, 0.0).astype(BF16), legendre_ref[first])
            + dot(jnp.where(from_second, 1.0, 0.0).astype(BF16), legendre_ref[second])
        ).astype(BF16)
        lat_in = lax.broadcasted_iota(jnp.int32, (nlat, hold), 0)
        lat_out = lax.broadcasted_iota(jnp.int32, (nlat, hold), 1)
        pack_send[...] = dot(packed, jnp.where(lat_in == lat_out + (1 - side) * hold, 1.0, 0.0).astype(BF16)).astype(BF16)
        packed_near = dot(packed, jnp.where(lat_in == lat_out + side * hold, 1.0, 0.0).astype(BF16)).astype(BF16)
        twice = jnp.where(
            lax.broadcasted_iota(jnp.int32, (high, tall), 0) // 2 == lax.broadcasted_iota(jnp.int32, (high, tall), 1),
            1.0, 0.0,
        ).astype(BF16)
        quad = jnp.where(
            lax.broadcasted_iota(jnp.int32, (hold, 4 * hold), 1) // 4 == lax.broadcasted_iota(jnp.int32, (hold, 4 * hold), 0),
            1.0, 0.0,
        ).astype(BF16)
        line_id = lax.broadcasted_iota(jnp.int32, (high, 4 * hold), 0)
        cell_id = lax.broadcasted_iota(jnp.int32, (high, 4 * hold), 1)

        def widen(block, lead):
            full = dot(dot(twice, block).astype(BF16), quad)
            in_second = jnp.where(line_id // 2 < lead, 0, 1)
            match = (cell_id % 2 == line_id % 2) & (cell_id % 4 // 2 == in_second)
            return jnp.where(match, full, 0.0).astype(BF16)

        pack_own[...] = widen(packed_near, lead)
        packed_full = dot(twice, packed).astype(BF16)
        pick(relay)
        near_recv[0, pl.ds(spot, 1)] = send[relay, pl.ds(me, 1)]
        near_recv[1, pl.ds(spot, 1)] = send[relay, pl.ds(mate, 1)]

    pick(direct[0])
    pl.semaphore_wait(barrier, others)

    if relay is not None:
        copy_to(mate, pack_send, pack_recv, pack_sems)
        to_near(lambda there: send.at[relay, side * near + there], near_recv.at[0, spot], fwd_sems.at[relay])
        to_near(lambda there: send.at[relay, (1 - side) * near + there], near_recv.at[1, spot], fwd_sems.at[relay])
    start_forward(direct[0])

    squares = jnp.zeros((8, chans), F32)
    for a in range(lat_dev):
        values = field_v[a].astype(F32)
        squares = squares + jnp.sum((values * values).reshape(width // 8, 8, chans), axis=0)
    square = jnp.sum(squares, axis=0, keepdims=True)
    own = jnp.concatenate([sums, square], axis=0)
    stat_src[...] = own
    stat_recv[pl.ds(me, 1)] = own[None]
    to_all(lambda to: stat_src, stat_recv.at[me], stat_sems)

    for k in direct[1:]:
        pick(k)

    if relay is not None:
        wait_bytes(pack_recv, pack_sems.at[1])
        pack_mate[...] = widen(pack_recv[...], degs - wave_ref[mate * slot_dev + first])
        wait_bytes(near_recv.at[:, pl.ds(0, near - 1)], fwd_sems.at[relay, 1])
        part_send[...] = dot(pack_mate[...], merged(near_recv[1])).reshape(part_send.shape).astype(BF16)
        copy_to(mate, part_send, part_recv, part_sems)

    for k in direct[1:]:
        start_forward(k)

    slot_a = lax.broadcasted_iota(jnp.int32, (slots, slots), 0)
    slot_b = lax.broadcasted_iota(jnp.int32, (slots, slots), 1)
    wave_col = jnp.sum(jnp.where(slot_a == slot_b, wave_row, 0.0), axis=1, keepdims=True)
    lane = lax.broadcasted_iota(jnp.int32, (1, rows), 1)
    slot_line = lax.broadcasted_iota(jnp.int32, (slots, rows), 0)
    place_line = lax.broadcasted_iota(jnp.int32, (4 * pad, rows), 0).astype(F32)

    def place_of(k):
        slot_of = lane // 8 * slot_dev + 2 * k + lane % 4 // 2
        wave_of = jnp.sum(jnp.where(slot_line == slot_of, wave_col, 0.0), axis=0, keepdims=True)
        target = wave_of + ((lane % 8 // 4 * 2 + lane % 2) * pad).astype(F32)
        return jnp.where(place_line == target, 1.0, 0.0).astype(BF16)

    place[...] = place_of(final)

    col = lax.broadcasted_iota(jnp.int32, (nlat, 4 * nlat), 1)
    lat_row = lax.broadcasted_iota(jnp.int32, (nlat, 4 * nlat), 0)
    degree = lax.broadcasted_iota(jnp.int32, (degs, nlat), 0)
    for k in direct:
        for jj in range(2):
            slot = 2 * k + jj
            wave = wave_ref[me * slot_dev + slot]
            kept = jnp.where(degree >= wave, legendre_ref[slot].astype(F32), 0.0).astype(BF16)
            for r in range(2):
                q = 2 * jj + r
                spread = jnp.where(col == 4 * lat_row + q, 1.0, 0.0).astype(BF16)
                lbig[slot_at[k], q * degs : (q + 1) * degs, :] = dot(kept, spread).astype(BF16)

    wait_bytes(stat_recv.at[pl.ds(0, others)], stat_sems.at[1])
    stats = stat_recv[...]
    total = jnp.sum(stats, axis=0)
    mean = total[0:1] / total_cells
    var = total[1:2] / total_cells - mean * mean
    scale = gain_ref[...] / jnp.sqrt(var + 1e-05)
    shift = (stats[:, 0, :] / float(lat_dev * width) - mean).astype(BF16)

    def owner_rows(copies):
        owner = lax.broadcasted_iota(jnp.int32, (copies * nlat, count), 1)
        lat_of = lax.broadcasted_iota(jnp.int32, (copies * nlat, count), 0)
        span = copies * lat_dev
        owned = jnp.where((lat_of >= owner * span) & (lat_of < (owner + 1) * span), 1.0, 0.0)
        return dot(owned.astype(BF16), shift).astype(BF16)

    mode_scale = scale * inv_root
    lanes = lax.broadcasted_iota(jnp.int32, (1, 2 * pad), 1)
    back_scale = math.sqrt(nlat / degs) * inv_root

    def table_sum(wave, r):
        return jnp.sum(jnp.where(lanes == wave + r * pad, tsum_row_ref[...], 0.0), axis=1, keepdims=True)

    def normalize(a):
        field_v[a] = ((field_v[a].astype(F32) - mean) * scale).astype(BF16)

    normalized = [0]

    def normalize_some(number):
        for a in range(normalized[0], min(lat_dev, normalized[0] + number)):
            normalize(a)
        normalized[0] = min(lat_dev, normalized[0] + number)

    if relay is not None:
        partial = dot(pack_own[...], merged(near_recv[0]))
        offset = dot(packed_full, owner_rows(1))
        line = lax.broadcasted_iota(jnp.int32, (high, 1), 0)
        is_first = line // 2 < lead
        is_real = line % 2 == 0
        waves = [wave_ref[me * slot_dev + first], wave_ref[me * slot_dev + second]]
        sums_of = [jnp.where(is_real, table_sum(w, 0), table_sum(w, 1)) for w in waves]
        partial = partial + jnp.where(is_first, sums_of[0], sums_of[1]) * offset
        weight = jnp.where(is_first, jnp.where(waves[0] == 0, 1.0, 2.0), jnp.where(waves[1] == 0, 1.0, 2.0)) * back_scale
        turn_a = lax.broadcasted_iota(jnp.int32, (high, high), 0)
        turn_b = lax.broadcasted_iota(jnp.int32, (high, high), 1)
        turn = jnp.where(
            (turn_a % 2 == 0) & (turn_b == turn_a + 1), -1.0, jnp.where((turn_a % 2 == 1) & (turn_b == turn_a - 1), 1.0, 0.0)
        ).astype(BF16)
        normalize_some(1)
        wait_bytes(part_recv, part_sems.at[1])
        both = ((partial + part_recv[...].astype(F32).reshape(high, chans)) * mode_scale).astype(BF16)
        turned = dot(turn, both).astype(BF16)
        of_slot = [dot(both, mix_v[s, 0]) + dot(turned, mix_v[s, 1]) for s in (first, second)]
        mixed = (jnp.where(is_first, of_slot[0], of_slot[1]) * weight).astype(BF16)
        mixed_send[...] = mixed.astype(F32).reshape(mixed_send.shape).astype(BF16)
        copy_to(mate, mixed_send, mixed_recv, mixed_sems)

        def expand(which, pack, block):
            back = lax.dot_general(pack, block, (((0,), (0,)), ((), ())), preferred_element_type=F32)
            near_back[which] = back.reshape(near, lat_pairs, 8, chans).astype(BF16)
            owner = me if which == 0 else mate
            ret[relay, pl.ds(owner, 1)] = near_back[which, pl.ds(spot, 1)]
            to_near(lambda there: near_back.at[which, there], ret.at[relay, owner], near_sems.at[which])

        expand(0, pack_own[...], mixed)

    shift_lat = owner_rows(4)

    for k in direct:
        i = slot_at[k]
        normalize_some(3)
        wait_bytes(recv.at[i, pl.ds(0, others)], fwd_sems.at[k, 1])
        arrived = merged(recv[i])
        coef = dot(lbig[i], arrived)
        offset = dot(lbig[i], shift_lat)
        mixed = []
        for jj in range(2):
            slot = 2 * k + jj
            wave = wave_ref[me * slot_dev + slot]
            parts = []
            for r in range(2):
                q = slice((2 * jj + r) * degs, (2 * jj + r + 1) * degs)
                parts.append(((coef[q] + table_sum(wave, r) * offset[q]) * mode_scale).astype(BF16))
            both = jnp.concatenate(parts, axis=0)
            by_real = dot(both, mix_v[slot, 0])
            by_imag = dot(both, mix_v[slot, 1])
            weight = jnp.where(wave == 0, 1.0, 2.0) * back_scale
            mixed.append(((by_real[:degs] - by_imag[degs:]) * weight).astype(BF16))
            mixed.append(((by_imag[:degs] + by_real[degs:]) * weight).astype(BF16))
        mixed = jnp.concatenate(mixed, axis=0)
        back = lax.dot_general(lbig[i], mixed, (((0,), (0,)), ((), ())), preferred_element_type=F32)
        back_send[i] = back.reshape(count, lat_pairs, 8, chans).astype(BF16)
        ret[k, pl.ds(me, 1)] = back_send[i, pl.ds(me, 1)]
        if k != final:
            to_all(lambda to: back_send.at[i, to], ret.at[k, me], back_sems.at[k])
        else:
            to_all(lambda to: back_send.at[i, to, 0], ret.at[k, me, 0], last_sems.at[0])

    if relay is not None:
        wait_bytes(mixed_recv, mixed_sems.at[1])
        expand(1, pack_mate[...], mixed_recv[...].astype(F32).reshape(high, chans).astype(BF16))
    for p in range(1, lat_pairs):
        to_all(lambda to: back_send.at[slot_at[final], to, p], ret.at[final, me, p], last_sems.at[p])
    normalize_some(lat_dev)

    wait_bytes(stat_recv.at[pl.ds(0, others)], stat_sems.at[0])
    for k in direct:
        wait_bytes(recv.at[slot_at[k], pl.ds(0, others)], fwd_sems.at[k, 0])
    if relay is not None:
        wait_bytes(near_recv.at[:, pl.ds(0, near - 1)], fwd_sems.at[relay, 0])
        wait_bytes(pack_recv, pack_sems.at[0])
        wait_bytes(part_recv, part_sems.at[0])
        wait_bytes(mixed_recv, mixed_sems.at[0])
        for which in range(2):
            wait_bytes(ret.at[relay, pl.ds(0, near - 1)], near_sems.at[which, 0])
    for k in direct[:-1]:
        wait_bytes(ret.at[k, pl.ds(0, others)], back_sems.at[k, 0])
        wait_bytes(ret.at[k, pl.ds(0, others)], back_sems.at[k, 1])
    if relay is not None:
        for which in range(2):
            wait_bytes(ret.at[relay, pl.ds(0, near - 1)], near_sems.at[which, 1])
    for k in range(groups):
        if k == final:
            continue
        spot_of = place_of(k)
        for p in range(lat_pairs):
            early = dot(spot_of, merged(ret[k, :, p])).reshape(2, half, chans)
            so_far = slice(2 * p, 2 * p + 2)
            raw[so_far] = early if k == 0 else raw[so_far] + early
    for p in range(lat_pairs):
        wait_bytes(ret.at[final, pl.ds(0, others), p], last_sems.at[p, 0])
        wait_bytes(ret.at[final, pl.ds(0, others), p], last_sems.at[p, 1])
        placed = dot(place[...], merged(ret[final, :, p]))
        if groups > 1:
            placed = placed + raw[2 * p : 2 * p + 2].reshape(4 * pad, chans)
        placed = placed.astype(BF16)
        if p < lat_pairs - 1:
            for parity in range(2):
                a = 2 * p + parity
                filtered = dot(back_table[...], placed[parity * half : (parity + 1) * half])
                field_v[a] = (field_v[a].astype(F32) + filtered).astype(BF16)
        else:
            placed_ref[...] = placed


def finish_kernel(part_ref, placed_ref, back_table_ref, out_hbm, tail, sems):
    lat_dev = part_ref.shape[0]
    half = placed_ref.shape[0] // 2
    copies = []
    for a in range(lat_dev - 2):
        copies.append(pltpu.make_async_copy(part_ref.at[a], out_hbm.at[a], sems.at[a]))
        copies[-1].start()
    for parity in range(2):
        a = lat_dev - 2 + parity
        filtered = dot(back_table_ref[...], placed_ref[parity * half : (parity + 1) * half])
        tail[parity] = (part_ref[a].astype(F32) + filtered).astype(BF16)
        copies.append(pltpu.make_async_copy(tail.at[parity], out_hbm.at[a], sems.at[a]))
        copies[-1].start()
    for copy in copies:
        copy.wait()


def per_device(field, gain, slot_wave, legendre, mixing):
    count = lax.axis_size("lat")
    lat_dev, width, chans = field.shape
    slot_dev, degs, nlat = legendre.shape
    groups, lat_pairs = slot_dev // 2, lat_dev // 2
    table, pad = wave_table(degs, width)
    tsum = table.astype(np.float64).sum(axis=1).astype(np.float32)
    back_table = jnp.asarray(table.T.copy())
    rows = count * 8
    near = count // 2
    kept_rows = packed_rows(groups - 1, count, slot_dev, degs)
    relay = groups - 1 if groups > 1 and 0 < kept_rows < nlat else None
    kept_rows = kept_rows if relay is not None else 8
    high = -(-2 * kept_rows // 8) * 8
    tall = -(-kept_rows // 16) * 16
    straight = groups - (relay is not None)
    vmem = pl.BlockSpec(memory_space=pltpu.VMEM)
    hbm = pl.BlockSpec(memory_space=pltpu.HBM)
    dma = pltpu.SemaphoreType.DMA
    half_limit = 30 * 2**20
    chunk = (lat_pairs, 8, chans)
    part, placed = pl.pallas_call(
        functools.partial(exchange_kernel, count, pad, relay, kept_rows),
        out_shape=(
            jax.ShapeDtypeStruct(field.shape, BF16),
            jax.ShapeDtypeStruct((4 * pad, chans), BF16),
        ),
        in_specs=[hbm] * 9,
        out_specs=(vmem, vmem),
        scratch_shapes=[
            pltpu.SMEM(slot_wave.shape, jnp.int32),
            pltpu.VMEM((1,) + slot_wave.shape, jnp.int32),
            pltpu.VMEM((1, chans), F32),
            pltpu.VMEM(table.shape, BF16),
            pltpu.VMEM((1, 2 * pad), F32),
            pltpu.VMEM(legendre.shape, BF16),
            pltpu.VMEM(mixing.shape, BF16),
            pltpu.VMEM(back_table.shape, BF16),
            pltpu.VMEM((groups, rows, 4 * pad), BF16),
            pltpu.VMEM((lat_dev, 2 * pad, chans), F32),
            pltpu.VMEM((lat_pairs, 4 * pad, chans), BF16),
            pltpu.VMEM((groups, count) + chunk, BF16),
            pltpu.VMEM((straight, count) + chunk, BF16),
            pltpu.VMEM((straight, count) + chunk, BF16),
            pltpu.VMEM((groups, count) + chunk, BF16),
            pltpu.VMEM((2, chans), F32),
            pltpu.VMEM((count, 2, chans), F32),
            pltpu.VMEM((straight, 4 * degs, 4 * nlat), BF16),
            pltpu.VMEM((4 * pad, rows), BF16),
            pltpu.VMEM((2, near) + chunk, BF16),
            pltpu.VMEM((2, near) + chunk, BF16),
            pltpu.VMEM((high // 8, 8, chans), BF16),
            pltpu.VMEM((high // 8, 8, chans), BF16),
            pltpu.VMEM((high // 8, 8, chans), BF16),
            pltpu.VMEM((high // 8, 8, chans), BF16),
            pltpu.VMEM((tall, nlat // 2), BF16),
            pltpu.VMEM((tall, nlat // 2), BF16),
            pltpu.VMEM((high, 2 * nlat), BF16),
            pltpu.VMEM((high, 2 * nlat), BF16),
            dma((lat_dev,)),
            dma((8,)),
            dma((2,)),
            dma((groups, 2)),
            dma((groups, 2)),
            dma((lat_pairs, 2)),
            dma((2,)),
            dma((2,)),
            dma((2,)),
            dma((2, 2)),
        ],
        compiler_params=pltpu.CompilerParams(
            collective_id=0, has_side_effects=True, vmem_limit_bytes=half_limit if count <= 16 else 63 * 2**20
        ),
        name="exchange",
    )(*(pltpu.with_memory_space_constraint(x, pltpu.HBM) for x in (
        field, slot_wave, slot_wave.reshape(1, -1), gain.reshape(1, chans), jnp.asarray(table),
        jnp.asarray(tsum.reshape(1, -1)), legendre, mixing, back_table,
    )))
    return pl.pallas_call(
        finish_kernel,
        out_shape=jax.ShapeDtypeStruct(field.shape, BF16),
        in_specs=[vmem, vmem, vmem],
        out_specs=hbm,
        scratch_shapes=[pltpu.VMEM((2, width, chans), BF16), dma((lat_dev,))],
        compiler_params=pltpu.CompilerParams(vmem_limit_bytes=half_limit),
        name="finish",
    )(part, placed, back_table)


def solution(mesh):
    return jax.shard_map(
        per_device,
        mesh=mesh,
        in_specs=(
            P(("member", "lat"), None, None),
            P(),
            P(),
            P("lat", None, None),
            P("lat", None, None, None),
        ),
        out_specs=P(("member", "lat"), None, None),
        check_vma=False,
    )
```

time: 42.5 us -> 36.6 us (0.86)
  Pallas kernels: 42.4 us -> 36.4 us
    pallas_call x2, Pallas kernels: 42.4 us -> 36.4 us  [the longest x1 34.3 us: per_device(): pl.pallas_call(functools.partial(exchange_kernel, count, pad, relay, kept...]
where the time goes in v1:
time: 36.6 us; the launch traced here: 36.5 us
  Pallas kernels  36.4 us (99%)
    pallas_call x1, Pallas kernels, per_device(): pl.pallas_call(functools.partial(exchange_kernel, count, pad, relay, kept...  34.3 us
    pallas_call x1, Pallas kernels, per_device(): pl.pallas_call(finish_kernel, out_shape=jax.ShapeDtypeStruct(field.shape,...  2.15 us

profile of v1, /device:TPU:0, one launch (start us, length us, event | category | flops | bytes accessed | tf_op | source)
XLA Modules:
  0.0 36.5 jit_solution(3667808291431084551)
XLA Ops:
  0.0 0.0 copy-start
  0.0 34.3 %exchange.1 = (bf16[6,1440,256]{2,1,0:T(8,128)(2,1)S(1)}, bf16[512,256]{1,0:T(8,128)(2,1)S(1)}) custom-call(bf16[6,1440,256]{2,1,0:T(8,128)(2,1)} %field_ref.1, s32[96]{0:T(128)} %wave_hbm.1, s32[1,96]{1,0:T(1,128)} %bitcast.2, f32[1,256]{1,0:T(1,128)} %bitcast.3, bf16[256,1440]{1,0:T(8,128)(2,1)} %constant.7.clone.table_hbm, ...), custom_call_target="tpu_custom_call" | custom-call | tf_op jit(solution)/shard_map/exchange/pallas_call | solution.py:460
  34.3 0.0 copy-done
  34.3 2.1 %finish.1 = bf16[6,1440,256]{2,1,0:T(8,128)(2,1)} custom-call(bf16[6,1440,256]{2,1,0:T(8,128)(2,1)S(1)} %get-tuple-element.7.part_ref, bf16[512,256]{1,0:T(8,128)(2,1)S(1)} %get-tuple-element.8.placed_ref, bf16[1440,256]{1,0:T(8,128)(2,1)S(1)} %copy-done), custom_call_target="tpu_custom_call" | custom-call | tf_op jit(solution)/shard_map/finish/pallas_call | solution.py:517
Async XLA Ops:
  0.0 34.3 %copy-start = (bf16[1440,256]{1,0:T(8,128)(2,1)S(1)}, bf16[1440,256]{1,0:T(8,128)(2,1)}, u32[]{:S(2)}) copy-start(bf16[1440,256]{1,0:T(8,128)(2,1)} %constant.6.clone.back_table_hbm.back_table_ref) | copy-start | bytes 2211844

commit v2 on v1

--- a/solution.py
+++ b/solution.py
@@ -14,13 +14,14 @@
 BF16 = jnp.bfloat16
 
 
-def wave_table(degs, width):
-    pad = -(-(degs + 1) // 128) * 128
-    waves = np.arange(degs + 1)[:, None]
+def wave_table(degs, slots, width):
+    kept = degs if slots == degs and degs % 32 == 0 else degs + 1
+    pad = degs if kept == degs else -(-kept // 128) * 128
+    waves = np.arange(kept)[:, None]
     phase = (waves * np.arange(width)[None, :] % width) * (2.0 * np.pi / width)
     table = np.zeros((2, pad, width), np.float32)
-    table[0, : degs + 1] = np.cos(phase)
-    table[1, : degs + 1] = -np.sin(phase)
+    table[0, :kept] = np.cos(phase)
+    table[1, :kept] = -np.sin(phase)
     return table.reshape(2 * pad, width).astype(BF16), pad
 
 
@@ -52,9 +53,9 @@
     relay,
     kept_rows,
     field_ref, wave_hbm, wave_row_hbm, gain_hbm, table_hbm, tsum_hbm, legendre_hbm, mixing_hbm, back_table_hbm,
-    field_v, placed_ref,
+    field_v, early_ref, block_ref, place,
     wave_ref, wave_row_ref, gain_ref, table_ref, tsum_row_ref, legendre_ref, mix_v, back_table,
-    select, raw, spec, send, recv, back_send, ret, stat_src, stat_recv, lbig, place,
+    select, raw, spec, send, recv, back_send, ret, stat_src, stat_recv, lbig,
     near_recv, near_back, part_send, part_recv, mixed_send, mixed_recv, pack_send, pack_recv, pack_own, pack_mate,
     field_sem, load_sem, stat_sems, fwd_sems, back_sems, last_sems, pack_sems, part_sems, mixed_sems, near_sems,
 ):
@@ -75,11 +76,44 @@
     order = ([relay] if relay is not None else []) + direct
     slot_at = {k: i for i, k in enumerate(direct)}
 
+    flips = [2**bit * (1 - 2 * lax.rem(me // 2**bit, 2)) for bit in range(count.bit_length() - 1)]
+
+    def peer(step):
+        if count & (count - 1):
+            return lax.rem(me + step, count)
+        to = me
+        for bit, flip in enumerate(flips):
+            to = to + flip if step >> bit & 1 else to
+        return to
+
+    def each_peer(act):
+        if count > 16:
+            lax.fori_loop(1, count, lambda step, carry: (act(partner(me, count - step, count)), carry)[1], 0)
+        else:
+            for step in range(count - 1, 0, -1):
+                act(peer(step))
+
+    def each_near(act):
+        if count > 16 or count & (count - 1):
+            lax.fori_loop(1, near, lambda step, carry: (act(side * near + partner(spot, near - step, near)), carry)[1], 0)
+        else:
+            for step in range(near - 1, 0, -1):
+                act(peer(step))
+
+    def each_far(act):
+        if count > 16 or count & (count - 1):
+            lax.fori_loop(0, near, lambda step, carry: (act((1 - side) * near + lax.rem(spot + step, near)), carry)[1], 0)
+        else:
+            for step in range(count - 1, near - 1, -1):
+                act(peer(step))
+
+    inner = side != spot // max(1, near // 2)
     barrier = pltpu.get_barrier_semaphore()
 
-    def greet(step, carry):
-        pl.semaphore_signal(barrier, inc=1, device_id={"lat": partner(me, step, count)}, device_id_type=MESH)
-        return carry
+    def greet(to):
+        pl.semaphore_signal(barrier, inc=1, device_id={"lat": to}, device_id_type=MESH)
+
+    each_peer(greet)
 
     def load_of(index, source, target):
         load = pltpu.make_async_copy(source, target, load_sem.at[index])
@@ -101,7 +135,6 @@
         load_of(6, mixing_hbm, mix_v),
         load_of(7, back_table_hbm, back_table),
     ]
-    lax.fori_loop(1, count, greet, 0)
 
     def copy_to(to, source, target, sems):
         pltpu.make_async_remote_copy(
@@ -110,20 +143,10 @@
         ).start()
 
     def to_all(source, target, sems):
-        def body(step, carry):
-            to = partner(me, count - step, count)
-            copy_to(to, source(to), target, sems)
-            return carry
-
-        lax.fori_loop(1, count, body, 0)
+        each_peer(lambda to: copy_to(to, source(to), target, sems))
 
     def to_near(source, target, sems):
-        def body(step, carry):
-            there = partner(spot, near - step, near)
-            copy_to(side * near + there, source(there), target, sems)
-            return carry
-
-        lax.fori_loop(1, near, body, 0)
+        each_near(lambda to: copy_to(to, source(to - side * near), target, sems))
 
     def wait_bytes(ref, sem):
         pltpu.make_async_copy(ref, ref, sem).wait()
@@ -148,50 +171,104 @@
     part_b = lax.broadcasted_iota(jnp.int32, (2 * pad, 2 * pad), 1)
     tsum_col = jnp.sum(jnp.where(part_a == part_b, tsum_row_ref[...], 0.0), axis=1, keepdims=True)
     table_load.wait()
+    half = 2 * pad
+
+    def pick(k, p):
+        picked = dot(select[k], spec[p])
+        send[k, :, p] = picked.reshape(count, 8, chans).astype(BF16)
+
+    def start_forward(k, pairs):
+        i = slot_at[k]
+        recv[i, pl.ds(me, 1), pairs] = send[k, pl.ds(me, 1), pairs]
+        to_all(lambda to: send.at[k, to, pairs], recv.at[i, me, pairs], fwd_sems.at[k])
+
+    def start_ahead(pairs):
+        i = slot_at[final]
+
+        @pl.when(inner)
+        def _():
+            each_far(lambda to: copy_to(to, send.at[final, to, pairs], recv.at[i, me, pairs], fwd_sems.at[final]))
+
+    def start_rest():
+        i = slot_at[final]
+        recv[i, pl.ds(me, 1)] = send[final, pl.ds(me, 1)]
+
+        @pl.when(jnp.logical_not(inner))
+        def _():
+            each_far(lambda to: copy_to(to, send.at[final, to], recv.at[i, me], fwd_sems.at[final]))
+
+        to_near(lambda there: send.at[final, side * near + there], recv.at[i, me], fwd_sems.at[final])
+
+    def start_near(pairs):
+        near_recv[0, pl.ds(spot, 1), pairs] = send[relay, pl.ds(me, 1), pairs]
+        near_recv[1, pl.ds(spot, 1), pairs] = send[relay, pl.ds(mate, 1), pairs]
+        to_near(lambda there: send.at[relay, side * near + there, pairs], near_recv.at[0, spot, pairs], fwd_sems.at[relay])
+        to_near(
+            lambda there: send.at[relay, (1 - side) * near + there, pairs], near_recv.at[1, spot, pairs], fwd_sems.at[relay]
+        )
+
     sums = jnp.zeros((1, chans), F32)
-    for a in range(lat_dev):
-        loads[a].wait()
-        raw[a] = dot(table_ref[...], field_v[a])
-        sums = sums + raw[a, 0:1, :]
-    local_mean = sums / float(lat_dev * width)
-
-    half = 2 * pad
+    squares = jnp.zeros((8, chans), F32)
     for p in range(lat_pairs):
+        for a in (2 * p, 2 * p + 1):
+            loads[a].wait()
+            raw[a] = dot(table_ref[...], field_v[a])
+            sums = sums + raw[a, 0:1, :]
+            values = field_v[a].astype(F32)
+            squares = squares + jnp.sum((values * values).reshape(width // 8, 8, chans), axis=0)
+        if p == 0:
+            anchor = sums / float(2 * width)
         for parity in range(2):
-            spec[p, parity * half : (parity + 1) * half, :] = (
-                raw[2 * p + parity] - tsum_col * local_mean
-            ).astype(BF16)
-
-    def pick(k):
-        for p in range(lat_pairs):
-            picked = dot(select[k], spec[p])
-            send[k, :, p] = picked.reshape(count, 8, chans).astype(BF16)
-
-    def start_forward(k):
-        i = slot_at[k]
-        recv[i, pl.ds(me, 1)] = send[k, pl.ds(me, 1)]
-        to_all(lambda to: send.at[k, to], recv.at[i, me], fwd_sems.at[k])
-
-    for load in late:
-        load.wait()
+            spec[p, parity * half : (parity + 1) * half, :] = (raw[2 * p + parity] - tsum_col * anchor).astype(BF16)
+        for k in order[:-1] if len(order) > 1 else order:
+            pick(k, p)
+        if p == 0:
+            pl.semaphore_wait(barrier, others)
+        if p == lat_pairs - 1:
+            own = jnp.concatenate([sums, jnp.sum(squares, axis=0, keepdims=True), anchor], axis=0)
+            stat_src[...] = own
+            stat_recv[pl.ds(me, 1)] = own[None]
+            to_all(lambda to: stat_src, stat_recv.at[me], stat_sems)
+        one = pl.ds(p, 1)
+        if relay is not None:
+            start_near(one)
+        if direct[0] != final or len(order) == 1:
+            start_forward(direct[0], one)
+        for k in direct[1:-1]:
+            start_forward(k, one)
+        if len(order) > 1:
+            pick(order[-1], p)
+            if relay is not None:
+                start_ahead(one)
+            else:
+                start_forward(final, one)
+        if p == 0:
+            for load in late:
+                load.wait()
+            if relay is not None:
+                first, second = 2 * relay, 2 * relay + 1
+                high = pack_own.shape[0]
+                tall, hold = pack_send.shape
+                degree_at = lax.broadcasted_iota(jnp.int32, (tall, degs), 1)
+                degree_row = lax.broadcasted_iota(jnp.int32, (tall, degs), 0)
+                lead = degs - wave_ref[me * slot_dev + first]
+                from_first = (degree_row < lead) & (degree_at == degs - 1 - degree_row)
+                from_second = (
+                    (degree_row >= lead) & (degree_row < kept_rows) & (degree_at == degree_row + (degs - kept_rows))
+                )
+                packed = (
+                    dot(jnp.where(from_first, 1.0, 0.0).astype(BF16), legendre_ref[first])
+                    + dot(jnp.where(from_second, 1.0, 0.0).astype(BF16), legendre_ref[second])
+                ).astype(BF16)
+                lat_in = lax.broadcasted_iota(jnp.int32, (nlat, hold), 0)
+                lat_out = lax.broadcasted_iota(jnp.int32, (nlat, hold), 1)
+                far_lats = jnp.where(lat_in == lat_out + (1 - side) * hold, 1.0, 0.0).astype(BF16)
+                pack_send[...] = dot(packed, far_lats).astype(BF16)
+                copy_to(mate, pack_send, pack_recv, pack_sems)
 
     if relay is not None:
-        first, second = 2 * relay, 2 * relay + 1
-        high = pack_own.shape[0]
-        tall, hold = pack_send.shape
-        degree_at = lax.broadcasted_iota(jnp.int32, (tall, degs), 1)
-        degree_row = lax.broadcasted_iota(jnp.int32, (tall, degs), 0)
-        lead = degs - wave_ref[me * slot_dev + first]
-        from_first = (degree_row < lead) & (degree_at == degs - 1 - degree_row)
-        from_second = (degree_row >= lead) & (degree_row < kept_rows) & (degree_at == degree_row + (degs - kept_rows))
-        packed = (
-            dot(jnp.where(from_first, 1.0, 0.0).astype(BF16), legendre_ref[first])
-            + dot(jnp.where(from_second, 1.0, 0.0).astype(BF16), legendre_ref[second])
-        ).astype(BF16)
-        lat_in = lax.broadcasted_iota(jnp.int32, (nlat, hold), 0)
-        lat_out = lax.broadcasted_iota(jnp.int32, (nlat, hold), 1)
-        pack_send[...] = dot(packed, jnp.where(lat_in == lat_out + (1 - side) * hold, 1.0, 0.0).astype(BF16)).astype(BF16)
-        packed_near = dot(packed, jnp.where(lat_in == lat_out + side * hold, 1.0, 0.0).astype(BF16)).astype(BF16)
+        near_lats = jnp.where(lat_in == lat_out + side * hold, 1.0, 0.0).astype(BF16)
+        packed_near = dot(packed, near_lats).astype(BF16)
         twice = jnp.where(
             lax.broadcasted_iota(jnp.int32, (high, tall), 0) // 2 == lax.broadcasted_iota(jnp.int32, (high, tall), 1),
             1.0, 0.0,
@@ -211,41 +288,13 @@
 
         pack_own[...] = widen(packed_near, lead)
         packed_full = dot(twice, packed).astype(BF16)
-        pick(relay)
-        near_recv[0, pl.ds(spot, 1)] = send[relay, pl.ds(me, 1)]
-        near_recv[1, pl.ds(spot, 1)] = send[relay, pl.ds(mate, 1)]
-
-    pick(direct[0])
-    pl.semaphore_wait(barrier, others)
-
-    if relay is not None:
-        copy_to(mate, pack_send, pack_recv, pack_sems)
-        to_near(lambda there: send.at[relay, side * near + there], near_recv.at[0, spot], fwd_sems.at[relay])
-        to_near(lambda there: send.at[relay, (1 - side) * near + there], near_recv.at[1, spot], fwd_sems.at[relay])
-    start_forward(direct[0])
-
-    squares = jnp.zeros((8, chans), F32)
-    for a in range(lat_dev):
-        values = field_v[a].astype(F32)
-        squares = squares + jnp.sum((values * values).reshape(width // 8, 8, chans), axis=0)
-    square = jnp.sum(squares, axis=0, keepdims=True)
-    own = jnp.concatenate([sums, square], axis=0)
-    stat_src[...] = own
-    stat_recv[pl.ds(me, 1)] = own[None]
-    to_all(lambda to: stat_src, stat_recv.at[me], stat_sems)
-
-    for k in direct[1:]:
-        pick(k)
-
-    if relay is not None:
         wait_bytes(pack_recv, pack_sems.at[1])
         pack_mate[...] = widen(pack_recv[...], degs - wave_ref[mate * slot_dev + first])
         wait_bytes(near_recv.at[:, pl.ds(0, near - 1)], fwd_sems.at[relay, 1])
         part_send[...] = dot(pack_mate[...], merged(near_recv[1])).reshape(part_send.shape).astype(BF16)
-        copy_to(mate, part_send, part_recv, part_sems)
-
-    for k in direct[1:]:
-        start_forward(k)
+        for i in range(part_send.shape[0]):
+            copy_to(mate, part_send.at[i], part_recv.at[i], part_sems)
+        start_rest()
 
     slot_a = lax.broadcasted_iota(jnp.int32, (slots, slots), 0)
     slot_b = lax.broadcasted_iota(jnp.int32, (slots, slots), 1)
@@ -281,7 +330,7 @@
     mean = total[0:1] / total_cells
     var = total[1:2] / total_cells - mean * mean
     scale = gain_ref[...] / jnp.sqrt(var + 1e-05)
-    shift = (stats[:, 0, :] / float(lat_dev * width) - mean).astype(BF16)
+    shift = (stats[:, 2, :] - mean).astype(BF16)
 
     def owner_rows(copies):
         owner = lax.broadcasted_iota(jnp.int32, (copies * nlat, count), 1)
@@ -307,7 +356,14 @@
             normalize(a)
         normalized[0] = min(lat_dev, normalized[0] + number)
 
-    if relay is not None:
+    def expand(which, pack, block):
+        back = lax.dot_general(pack, block, (((0,), (0,)), ((), ())), preferred_element_type=F32)
+        near_back[which] = back.reshape(near, lat_pairs, 8, chans).astype(BF16)
+        owner = me if which == 0 else mate
+        ret[relay, pl.ds(owner, 1)] = near_back[which, pl.ds(spot, 1)]
+        to_near(lambda there: near_back.at[which, there], ret.at[relay, owner], near_sems.at[which])
+
+    def relay_step():
         partial = dot(pack_own[...], merged(near_recv[0]))
         offset = dot(packed_full, owner_rows(1))
         line = lax.broadcasted_iota(jnp.int32, (high, 1), 0)
@@ -322,29 +378,21 @@
         turn = jnp.where(
             (turn_a % 2 == 0) & (turn_b == turn_a + 1), -1.0, jnp.where((turn_a % 2 == 1) & (turn_b == turn_a - 1), 1.0, 0.0)
         ).astype(BF16)
-        normalize_some(1)
         wait_bytes(part_recv, part_sems.at[1])
         both = ((partial + part_recv[...].astype(F32).reshape(high, chans)) * mode_scale).astype(BF16)
         turned = dot(turn, both).astype(BF16)
         of_slot = [dot(both, mix_v[s, 0]) + dot(turned, mix_v[s, 1]) for s in (first, second)]
         mixed = (jnp.where(is_first, of_slot[0], of_slot[1]) * weight).astype(BF16)
         mixed_send[...] = mixed.astype(F32).reshape(mixed_send.shape).astype(BF16)
-        copy_to(mate, mixed_send, mixed_recv, mixed_sems)
-
-        def expand(which, pack, block):
-            back = lax.dot_general(pack, block, (((0,), (0,)), ((), ())), preferred_element_type=F32)
-            near_back[which] = back.reshape(near, lat_pairs, 8, chans).astype(BF16)
-            owner = me if which == 0 else mate
-            ret[relay, pl.ds(owner, 1)] = near_back[which, pl.ds(spot, 1)]
-            to_near(lambda there: near_back.at[which, there], ret.at[relay, owner], near_sems.at[which])
+        for i in range(mixed_send.shape[0]):
+            copy_to(mate, mixed_send.at[i], mixed_recv.at[i], mixed_sems)
 
         expand(0, pack_own[...], mixed)
 
     shift_lat = owner_rows(4)
 
-    for k in direct:
+    def direct_step(k):
         i = slot_at[k]
-        normalize_some(3)
         wait_bytes(recv.at[i, pl.ds(0, others)], fwd_sems.at[k, 1])
         arrived = merged(recv[i])
         coef = dot(lbig[i], arrived)
@@ -367,17 +415,25 @@
         back = lax.dot_general(lbig[i], mixed, (((0,), (0,)), ((), ())), preferred_element_type=F32)
         back_send[i] = back.reshape(count, lat_pairs, 8, chans).astype(BF16)
         ret[k, pl.ds(me, 1)] = back_send[i, pl.ds(me, 1)]
+        start_back(k, pl.ds(0, 1), last_sems.at[0] if k == final else back_sems.at[k])
+
+    def start_back(k, pairs, sems):
+        to_all(lambda to: back_send.at[slot_at[k], to, pairs], ret.at[k, me, pairs], sems)
+
+    rest = pl.ds(1, lat_pairs - 1)
+    for k in direct:
+        direct_step(k)
+        if relay is not None and k == direct[max(0, len(direct) - 2)]:
+            relay_step()
         if k != final:
-            to_all(lambda to: back_send.at[i, to], ret.at[k, me], back_sems.at[k])
-        else:
-            to_all(lambda to: back_send.at[i, to, 0], ret.at[k, me, 0], last_sems.at[0])
-
+            start_back(k, rest, back_sems.at[k])
+            normalize_some(2)
+    normalize_some(lat_dev)
     if relay is not None:
         wait_bytes(mixed_recv, mixed_sems.at[1])
         expand(1, pack_mate[...], mixed_recv[...].astype(F32).reshape(high, chans).astype(BF16))
     for p in range(1, lat_pairs):
-        to_all(lambda to: back_send.at[slot_at[final], to, p], ret.at[final, me, p], last_sems.at[p])
-    normalize_some(lat_dev)
+        start_back(final, pl.ds(p, 1), last_sems.at[p])
 
     wait_bytes(stat_recv.at[pl.ds(0, others)], stat_sems.at[0])
     for k in direct:
@@ -389,49 +445,57 @@
         wait_bytes(mixed_recv, mixed_sems.at[0])
         for which in range(2):
             wait_bytes(ret.at[relay, pl.ds(0, near - 1)], near_sems.at[which, 0])
-    for k in direct[:-1]:
-        wait_bytes(ret.at[k, pl.ds(0, others)], back_sems.at[k, 0])
-        wait_bytes(ret.at[k, pl.ds(0, others)], back_sems.at[k, 1])
-    if relay is not None:
+    begun = False
+    for k in direct[:-1] + ([relay] if relay is not None else []):
+        spot_of = place_of(k)
         for which in range(2):
-            wait_bytes(ret.at[relay, pl.ds(0, near - 1)], near_sems.at[which, 1])
-    for k in range(groups):
-        if k == final:
-            continue
-        spot_of = place_of(k)
+            if k != relay:
+                wait_bytes(ret.at[k, pl.ds(0, others)], back_sems.at[k, which])
+            else:
+                wait_bytes(ret.at[k, pl.ds(0, near - 1)], near_sems.at[which, 1])
         for p in range(lat_pairs):
             early = dot(spot_of, merged(ret[k, :, p])).reshape(2, half, chans)
             so_far = slice(2 * p, 2 * p + 2)
-            raw[so_far] = early if k == 0 else raw[so_far] + early
+            raw[so_far] = raw[so_far] + early if begun else early
+        begun = True
+    if not begun:
+        raw[...] = jnp.zeros(raw.shape, F32)
+    early_ref[...] = raw[lat_dev - 2 : lat_dev].reshape(4 * pad, chans)
     for p in range(lat_pairs):
         wait_bytes(ret.at[final, pl.ds(0, others), p], last_sems.at[p, 0])
         wait_bytes(ret.at[final, pl.ds(0, others), p], last_sems.at[p, 1])
-        placed = dot(place[...], merged(ret[final, :, p]))
-        if groups > 1:
-            placed = placed + raw[2 * p : 2 * p + 2].reshape(4 * pad, chans)
-        placed = placed.astype(BF16)
-        if p < lat_pairs - 1:
-            for parity in range(2):
-                a = 2 * p + parity
-                filtered = dot(back_table[...], placed[parity * half : (parity + 1) * half])
-                field_v[a] = (field_v[a].astype(F32) + filtered).astype(BF16)
-        else:
-            placed_ref[...] = placed
-
-
-def finish_kernel(part_ref, placed_ref, back_table_ref, out_hbm, tail, sems):
+        block = merged(ret[final, :, p])
+        if p == lat_pairs - 1:
+            block_ref[...] = block
+            continue
+        placed = (dot(place[...], block) + raw[2 * p : 2 * p + 2].reshape(4 * pad, chans)).astype(BF16)
+        for parity in range(2):
+            a = 2 * p + parity
+            filtered = dot(back_table[...], placed[parity * half : (parity + 1) * half])
+            field_v[a] = (field_v[a].astype(F32) + filtered).astype(BF16)
+
+
+def finish_kernel(part_ref, early_ref, block_ref, place_ref, back_table_ref, out_hbm, tail, sems):
     lat_dev = part_ref.shape[0]
-    half = placed_ref.shape[0] // 2
+    width = part_ref.shape[1]
+    half = place_ref.shape[0] // 2
+    pieces = 3 if width % 48 == 0 else 1
+    deep = width // pieces
     copies = []
     for a in range(lat_dev - 2):
         copies.append(pltpu.make_async_copy(part_ref.at[a], out_hbm.at[a], sems.at[a]))
         copies[-1].start()
+    placed = (dot(place_ref[...], block_ref[...]) + early_ref[...]).astype(BF16)
     for parity in range(2):
         a = lat_dev - 2 + parity
-        filtered = dot(back_table_ref[...], placed_ref[parity * half : (parity + 1) * half])
-        tail[parity] = (part_ref[a].astype(F32) + filtered).astype(BF16)
-        copies.append(pltpu.make_async_copy(tail.at[parity], out_hbm.at[a], sems.at[a]))
-        copies[-1].start()
+        for piece in range(pieces):
+            lines = pl.ds(piece * deep, deep)
+            filtered = dot(back_table_ref[lines, :], placed[parity * half : (parity + 1) * half])
+            tail[parity, lines] = (part_ref[a, lines].astype(F32) + filtered).astype(BF16)
+            copies.append(
+                pltpu.make_async_copy(tail.at[parity, lines], out_hbm.at[a, lines], sems.at[lat_dev + parity * pieces + piece])
+            )
+            copies[-1].start()
     for copy in copies:
         copy.wait()
 
@@ -441,7 +505,7 @@
     lat_dev, width, chans = field.shape
     slot_dev, degs, nlat = legendre.shape
     groups, lat_pairs = slot_dev // 2, lat_dev // 2
-    table, pad = wave_table(degs, width)
+    table, pad = wave_table(degs, count * slot_dev, width)
     tsum = table.astype(np.float64).sum(axis=1).astype(np.float32)
     back_table = jnp.asarray(table.T.copy())
     rows = count * 8
@@ -457,14 +521,16 @@
     dma = pltpu.SemaphoreType.DMA
     half_limit = 30 * 2**20
     chunk = (lat_pairs, 8, chans)
-    part, placed = pl.pallas_call(
+    part, early, block, place = pl.pallas_call(
         functools.partial(exchange_kernel, count, pad, relay, kept_rows),
         out_shape=(
             jax.ShapeDtypeStruct(field.shape, BF16),
-            jax.ShapeDtypeStruct((4 * pad, chans), BF16),
+            jax.ShapeDtypeStruct((4 * pad, chans), F32),
+            jax.ShapeDtypeStruct((rows, chans), BF16),
+            jax.ShapeDtypeStruct((4 * pad, rows), BF16),
         ),
         in_specs=[hbm] * 9,
-        out_specs=(vmem, vmem),
+        out_specs=(vmem,) * 4,
         scratch_shapes=[
             pltpu.SMEM(slot_wave.shape, jnp.int32),
             pltpu.VMEM((1,) + slot_wave.shape, jnp.int32),
@@ -481,10 +547,9 @@
             pltpu.VMEM((straight, count) + chunk, BF16),
             pltpu.VMEM((straight, count) + chunk, BF16),
             pltpu.VMEM((groups, count) + chunk, BF16),
-            pltpu.VMEM((2, chans), F32),
-            pltpu.VMEM((count, 2, chans), F32),
+            pltpu.VMEM((3, chans), F32),
+            pltpu.VMEM((count, 3, chans), F32),
             pltpu.VMEM((straight, 4 * degs, 4 * nlat), BF16),
-            pltpu.VMEM((4 * pad, rows), BF16),
             pltpu.VMEM((2, near) + chunk, BF16),
             pltpu.VMEM((2, near) + chunk, BF16),
             pltpu.VMEM((high // 8, 8, chans), BF16),
@@ -517,12 +582,12 @@
     return pl.pallas_call(
         finish_kernel,
         out_shape=jax.ShapeDtypeStruct(field.shape, BF16),
-        in_specs=[vmem, vmem, vmem],
+        in_specs=[vmem] * 5,
         out_specs=hbm,
-        scratch_shapes=[pltpu.VMEM((2, width, chans), BF16), dma((lat_dev,))],
+        scratch_shapes=[pltpu.VMEM((2, width, chans), BF16), dma((lat_dev + 6,))],
         compiler_params=pltpu.CompilerParams(vmem_limit_bytes=half_limit),
         name="finish",
-    )(part, placed, back_table)
+    )(part, early, block, place, back_table)
 
 
 def solution(mesh):

time: 36.6 us -> 33.5 us (0.915)
  Pallas kernels: 36.4 us -> 33.3 us
    pallas_call x1, Pallas kernels: 34.3 us -> 31.2 us  [per_device(): pl.pallas_call(functools.partial(exchange_kernel, count, pad, relay, kept...]
where the time goes in v2:
time: 33.5 us; the launch traced here: 33.4 us
  Pallas kernels  33.3 us (99%)
    pallas_call x1, Pallas kernels, per_device(): pl.pallas_call(functools.partial(exchange_kernel, count, pad, relay, kept...  31.2 us
    pallas_call x1, Pallas kernels, per_device(): pl.pallas_call(finish_kernel, out_shape=jax.ShapeDtypeStruct(field.shape,...  2.18 us

profile of v2, /device:TPU:0, one launch (start us, length us, event | category | flops | bytes accessed | tf_op | source)
XLA Modules:
  0.0 33.4 jit_solution(991776589994946193)
XLA Ops:
  0.0 0.0 copy-start
  0.0 31.2 %exchange.1 = (bf16[6,1440,256]{2,1,0:T(8,128)(2,1)S(1)}, f32[384,256]{1,0:T(8,128)S(1)}, bf16[128,256]{1,0:T(8,128)(2,1)S(1)}, bf16[384,128]{1,0:T(8,128)(2,1)S(1)}) custom-call(bf16[6,1440,256]{2,1,0:T(8,128)(2,1)} %field_ref.1, s32[96]{0:T(128)} %wave_hbm.1, s32[1,96]{1,0:T(1,128)} %bitcast.2, f32[1,256]{1,0:T(1,128)} %bitcast.3, ...), custom_call_target="tpu_custom_call" | custom-call | tf_op jit(solution)/shard_map/exchange/pallas_call | solution.py:524
  31.2 0.0 copy-done
  31.2 2.2 %finish.1 = bf16[6,1440,256]{2,1,0:T(8,128)(2,1)} custom-call(bf16[6,1440,256]{2,1,0:T(8,128)(2,1)S(1)} %get-tuple-element.9.part_ref, f32[384,256]{1,0:T(8,128)S(1)} %get-tuple-element.10.early_ref, bf16[128,256]{1,0:T(8,128)(2,1)S(1)} %get-tuple-element.11.block_ref, bf16[384,128]{1,0:T(8,128)(2,1)S(1)} %get-tuple-element.12.place_ref, ...), custom_call_target="tpu_custom_call" | custom-call | tf_op jit(solution)/shard_map/finish/pallas_call | solution.py:582
Async XLA Ops:
  0.0 31.2 %copy-start = (bf16[1440,192]{1,0:T(8,128)(2,1)S(1)}, bf16[1440,192]{1,0:T(8,128)(2,1)}, u32[]{:S(2)}) copy-start(bf16[1440,192]{1,0:T(8,128)(2,1)} %constant.6.clone.back_table_hbm.back_table_ref) | copy-start | bytes 1658884

commit v3 on v2

--- a/solution.py
+++ b/solution.py
@@ -55,7 +55,7 @@
     field_ref, wave_hbm, wave_row_hbm, gain_hbm, table_hbm, tsum_hbm, legendre_hbm, mixing_hbm, back_table_hbm,
     field_v, early_ref, block_ref, place,
     wave_ref, wave_row_ref, gain_ref, table_ref, tsum_row_ref, legendre_ref, mix_v, back_table,
-    select, raw, spec, send, recv, back_send, ret, stat_src, stat_recv, lbig,
+    select, raw, spec, send, recv, back_send, ret, stat_src, stat_recv, sum_send, sum_recv, gap_send, gap_recv, lbig,
     near_recv, near_back, part_send, part_recv, mixed_send, mixed_recv, pack_send, pack_recv, pack_own, pack_mate,
     field_sem, load_sem, stat_sems, fwd_sems, back_sems, last_sems, pack_sems, part_sems, mixed_sems, near_sems,
 ):
@@ -75,6 +75,7 @@
     final = direct[-1]
     order = ([relay] if relay is not None else []) + direct
     slot_at = {k: i for i, k in enumerate(direct)}
+    tails = block_ref.shape[0]
 
     flips = [2**bit * (1 - 2 * lax.rem(me // 2**bit, 2)) for bit in range(count.bit_length() - 1)]
 
@@ -195,7 +196,8 @@
 
         @pl.when(jnp.logical_not(inner))
         def _():
-            each_far(lambda to: copy_to(to, send.at[final, to], recv.at[i, me], fwd_sems.at[final]))
+            pairs = pl.ds(1, lat_pairs - 1)
+            each_far(lambda to: copy_to(to, send.at[final, to, pairs], recv.at[i, me, pairs], fwd_sems.at[final]))
 
         to_near(lambda there: send.at[final, side * near + there], recv.at[i, me], fwd_sems.at[final])
 
@@ -210,9 +212,12 @@
     sums = jnp.zeros((1, chans), F32)
     squares = jnp.zeros((8, chans), F32)
     for p in range(lat_pairs):
+        loads[2 * p].wait()
+        loads[2 * p + 1].wait()
+        two = dot(table_ref[...], jnp.concatenate([field_v[2 * p], field_v[2 * p + 1]], axis=1))
+        raw[2 * p] = two[:, :chans]
+        raw[2 * p + 1] = two[:, chans:]
         for a in (2 * p, 2 * p + 1):
-            loads[a].wait()
-            raw[a] = dot(table_ref[...], field_v[a])
             sums = sums + raw[a, 0:1, :]
             values = field_v[a].astype(F32)
             squares = squares + jnp.sum((values * values).reshape(width // 8, 8, chans), axis=0)
@@ -227,8 +232,8 @@
         if p == lat_pairs - 1:
             own = jnp.concatenate([sums, jnp.sum(squares, axis=0, keepdims=True), anchor], axis=0)
             stat_src[...] = own
-            stat_recv[pl.ds(me, 1)] = own[None]
-            to_all(lambda to: stat_src, stat_recv.at[me], stat_sems)
+            stat_recv[pl.ds(spot, 1)] = own[None]
+            to_near(lambda there: stat_src, stat_recv.at[spot], stat_sems.at[0])
         one = pl.ds(p, 1)
         if relay is not None:
             start_near(one)
@@ -267,6 +272,12 @@
                 copy_to(mate, pack_send, pack_recv, pack_sems)
 
     if relay is not None:
+
+        @pl.when(jnp.logical_not(inner))
+        def _():
+            pairs = pl.ds(0, 1)
+            each_far(lambda to: copy_to(to, send.at[final, to, pairs], recv.at[slot_at[final], me, pairs], fwd_sems.at[final]))
+
         near_lats = jnp.where(lat_in == lat_out + side * hold, 1.0, 0.0).astype(BF16)
         packed_near = dot(packed, near_lats).astype(BF16)
         twice = jnp.where(
@@ -288,14 +299,6 @@
 
         pack_own[...] = widen(packed_near, lead)
         packed_full = dot(twice, packed).astype(BF16)
-        wait_bytes(pack_recv, pack_sems.at[1])
-        pack_mate[...] = widen(pack_recv[...], degs - wave_ref[mate * slot_dev + first])
-        wait_bytes(near_recv.at[:, pl.ds(0, near - 1)], fwd_sems.at[relay, 1])
-        part_send[...] = dot(pack_mate[...], merged(near_recv[1])).reshape(part_send.shape).astype(BF16)
-        for i in range(part_send.shape[0]):
-            copy_to(mate, part_send.at[i], part_recv.at[i], part_sems)
-        start_rest()
-
     slot_a = lax.broadcasted_iota(jnp.int32, (slots, slots), 0)
     slot_b = lax.broadcasted_iota(jnp.int32, (slots, slots), 1)
     wave_col = jnp.sum(jnp.where(slot_a == slot_b, wave_row, 0.0), axis=1, keepdims=True)
@@ -324,20 +327,43 @@
                 spread = jnp.where(col == 4 * lat_row + q, 1.0, 0.0).astype(BF16)
                 lbig[slot_at[k], q * degs : (q + 1) * degs, :] = dot(kept, spread).astype(BF16)
 
-    wait_bytes(stat_recv.at[pl.ds(0, others)], stat_sems.at[1])
+    wait_bytes(stat_recv.at[pl.ds(0, near - 1)], stat_sems.at[0, 1])
     stats = stat_recv[...]
-    total = jnp.sum(stats, axis=0)
+    near_total = jnp.sum(stats[:, :2, :], axis=0)
+    sum_send[...] = near_total
+    gap_send[...] = (stats[:, 2, :] - near_total[0:1] / (0.5 * total_cells)).astype(BF16)
+    copy_to(mate, sum_send, sum_recv, stat_sems.at[1])
+    copy_to(mate, gap_send, gap_recv, stat_sems.at[2])
+
+    if relay is not None:
+        wait_bytes(pack_recv, pack_sems.at[1])
+        pack_mate[...] = widen(pack_recv[...], degs - wave_ref[mate * slot_dev + first])
+        wait_bytes(near_recv.at[:, pl.ds(0, near - 1)], fwd_sems.at[relay, 1])
+        part_send[...] = dot(pack_mate[...], merged(near_recv[1])).reshape(part_send.shape).astype(BF16)
+        for i in range(part_send.shape[0]):
+            copy_to(mate, part_send.at[i], part_recv.at[i], part_sems)
+        start_rest()
+
+    wait_bytes(sum_recv, stat_sems.at[1, 1])
+    wait_bytes(gap_recv, stat_sems.at[2, 1])
+    total = near_total + sum_recv[...]
     mean = total[0:1] / total_cells
     var = total[1:2] / total_cells - mean * mean
     scale = gain_ref[...] / jnp.sqrt(var + 1e-05)
-    shift = (stats[:, 2, :] - mean).astype(BF16)
+    shift_near = (stats[:, 2, :] - mean).astype(BF16)
+    shift_far = (gap_recv[...].astype(F32) + (sum_recv[0:1] / (0.5 * total_cells) - mean)).astype(BF16)
 
     def owner_rows(copies):
-        owner = lax.broadcasted_iota(jnp.int32, (copies * nlat, count), 1)
-        lat_of = lax.broadcasted_iota(jnp.int32, (copies * nlat, count), 0)
+        owner = lax.broadcasted_iota(jnp.int32, (copies * nlat, near), 1)
+        lat_of = lax.broadcasted_iota(jnp.int32, (copies * nlat, near), 0)
         span = copies * lat_dev
-        owned = jnp.where((lat_of >= owner * span) & (lat_of < (owner + 1) * span), 1.0, 0.0)
-        return dot(owned.astype(BF16), shift).astype(BF16)
+
+        def rows_of(first, shift):
+            start = (owner + first) * span
+            owned = jnp.where((lat_of >= start) & (lat_of < start + span), 1.0, 0.0)
+            return dot(owned.astype(BF16), shift)
+
+        return (rows_of(side * near, shift_near) + rows_of((1 - side) * near, shift_far)).astype(BF16)
 
     mode_scale = scale * inv_root
     lanes = lax.broadcasted_iota(jnp.int32, (1, 2 * pad), 1)
@@ -435,7 +461,9 @@
     for p in range(1, lat_pairs):
         start_back(final, pl.ds(p, 1), last_sems.at[p])
 
-    wait_bytes(stat_recv.at[pl.ds(0, others)], stat_sems.at[0])
+    wait_bytes(stat_recv.at[pl.ds(0, near - 1)], stat_sems.at[0, 0])
+    wait_bytes(sum_recv, stat_sems.at[1, 0])
+    wait_bytes(gap_recv, stat_sems.at[2, 0])
     for k in direct:
         wait_bytes(recv.at[slot_at[k], pl.ds(0, others)], fwd_sems.at[k, 0])
     if relay is not None:
@@ -460,13 +488,13 @@
         begun = True
     if not begun:
         raw[...] = jnp.zeros(raw.shape, F32)
-    early_ref[...] = raw[lat_dev - 2 : lat_dev].reshape(4 * pad, chans)
+    early_ref[...] = raw[lat_dev - 2 * tails : lat_dev].reshape(tails, 4 * pad, chans)
     for p in range(lat_pairs):
         wait_bytes(ret.at[final, pl.ds(0, others), p], last_sems.at[p, 0])
         wait_bytes(ret.at[final, pl.ds(0, others), p], last_sems.at[p, 1])
         block = merged(ret[final, :, p])
-        if p == lat_pairs - 1:
-            block_ref[...] = block
+        if p >= lat_pairs - tails:
+            block_ref[p - lat_pairs + tails] = block
             continue
         placed = (dot(place[...], block) + raw[2 * p : 2 * p + 2].reshape(4 * pad, chans)).astype(BF16)
         for parity in range(2):
@@ -482,20 +510,25 @@
     pieces = 3 if width % 48 == 0 else 1
     deep = width // pieces
     copies = []
-    for a in range(lat_dev - 2):
+    tails, chans = block_ref.shape[0], block_ref.shape[2]
+    done = lat_dev - 2 * tails
+    for a in range(done):
         copies.append(pltpu.make_async_copy(part_ref.at[a], out_hbm.at[a], sems.at[a]))
         copies[-1].start()
-    placed = (dot(place_ref[...], block_ref[...]) + early_ref[...]).astype(BF16)
-    for parity in range(2):
-        a = lat_dev - 2 + parity
-        for piece in range(pieces):
-            lines = pl.ds(piece * deep, deep)
-            filtered = dot(back_table_ref[lines, :], placed[parity * half : (parity + 1) * half])
-            tail[parity, lines] = (part_ref[a, lines].astype(F32) + filtered).astype(BF16)
-            copies.append(
-                pltpu.make_async_copy(tail.at[parity, lines], out_hbm.at[a, lines], sems.at[lat_dev + parity * pieces + piece])
-            )
-            copies[-1].start()
+    for t in range(tails):
+        placed = (dot(place_ref[...], block_ref[t]) + early_ref[t]).astype(BF16)
+        for parity in range(2):
+            a = done + 2 * t + parity
+            for piece in range(pieces):
+                lines = pl.ds(piece * deep, deep)
+                filtered = dot(back_table_ref[lines, :], placed[parity * half : (parity + 1) * half])
+                tail[2 * t + parity, lines] = (part_ref[a, lines].astype(F32) + filtered).astype(BF16)
+                copies.append(
+                    pltpu.make_async_copy(
+                        tail.at[2 * t + parity, lines], out_hbm.at[a, lines], sems.at[lat_dev + (2 * t + parity) * pieces + piece]
+                    )
+                )
+                copies[-1].start()
     for copy in copies:
         copy.wait()
 
@@ -516,6 +549,7 @@
     high = -(-2 * kept_rows // 8) * 8
     tall = -(-kept_rows // 16) * 16
     straight = groups - (relay is not None)
+    tails = min(2, lat_pairs)
     vmem = pl.BlockSpec(memory_space=pltpu.VMEM)
     hbm = pl.BlockSpec(memory_space=pltpu.HBM)
     dma = pltpu.SemaphoreType.DMA
@@ -525,8 +559,8 @@
         functools.partial(exchange_kernel, count, pad, relay, kept_rows),
         out_shape=(
             jax.ShapeDtypeStruct(field.shape, BF16),
-            jax.ShapeDtypeStruct((4 * pad, chans), F32),
-            jax.ShapeDtypeStruct((rows, chans), BF16),
+            jax.ShapeDtypeStruct((tails, 4 * pad, chans), F32),
+            jax.ShapeDtypeStruct((tails, rows, chans), BF16),
             jax.ShapeDtypeStruct((4 * pad, rows), BF16),
         ),
         in_specs=[hbm] * 9,
@@ -548,7 +582,11 @@
             pltpu.VMEM((straight, count) + chunk, BF16),
             pltpu.VMEM((groups, count) + chunk, BF16),
             pltpu.VMEM((3, chans), F32),
-            pltpu.VMEM((count, 3, chans), F32),
+            pltpu.VMEM((near, 3, chans), F32),
+            pltpu.VMEM((2, chans), F32),
+            pltpu.VMEM((2, chans), F32),
+            pltpu.VMEM((near, chans), BF16),
+            pltpu.VMEM((near, chans), BF16),
             pltpu.VMEM((straight, 4 * degs, 4 * nlat), BF16),
             pltpu.VMEM((2, near) + chunk, BF16),
             pltpu.VMEM((2, near) + chunk, BF16),
@@ -562,7 +600,7 @@
             pltpu.VMEM((high, 2 * nlat), BF16),
             dma((lat_dev,)),
             dma((8,)),
-            dma((2,)),
+            dma((3, 2)),
             dma((groups, 2)),
             dma((groups, 2)),
             dma((lat_pairs, 2)),
@@ -584,7 +622,7 @@
         out_shape=jax.ShapeDtypeStruct(field.shape, BF16),
         in_specs=[vmem] * 5,
         out_specs=hbm,
-        scratch_shapes=[pltpu.VMEM((2, width, chans), BF16), dma((lat_dev + 6,))],
+        scratch_shapes=[pltpu.VMEM((2 * tails, width, chans), BF16), dma((lat_dev + 6 * tails,))],
         compiler_params=pltpu.CompilerParams(vmem_limit_bytes=half_limit),
         name="finish",
     )(part, early, block, place, back_table)

time: 33.5 us -> 32.6 us (0.973)
  Pallas kernels: 33.3 us -> 32.4 us
    pallas_call x1, Pallas kernels: 31.2 us -> 30.1 us  [per_device(): pl.pallas_call(functools.partial(exchange_kernel, count, pad, relay, kept...]
where the time goes in v3:
time: 32.6 us; the launch traced here: 32.5 us
  Pallas kernels  32.4 us (99%)
    pallas_call x1, Pallas kernels, per_device(): pl.pallas_call(functools.partial(exchange_kernel, count, pad, relay, kept...  30.1 us
    pallas_call x1, Pallas kernels, per_device(): pl.pallas_call(finish_kernel, out_shape=jax.ShapeDtypeStruct(field.shape,...  2.34 us

profile of v3, /device:TPU:0, one launch (start us, length us, event | category | flops | bytes accessed | tf_op | source)
XLA Modules:
  0.0 32.5 jit_solution(11485492733757710173)
XLA Ops:
  0.0 0.0 copy-start
  0.0 30.1 %exchange.1 = (bf16[6,1440,256]{2,1,0:T(8,128)(2,1)S(1)}, f32[2,384,256]{2,1,0:T(8,128)S(1)}, bf16[2,128,256]{2,1,0:T(8,128)(2,1)S(1)}, bf16[384,128]{1,0:T(8,128)(2,1)S(1)}) custom-call(bf16[6,1440,256]{2,1,0:T(8,128)(2,1)} %field_ref.1, s32[96]{0:T(128)} %wave_hbm.1, s32[1,96]{1,0:T(1,128)} %bitcast.2, f32[1,256]{1,0:T(1,128)} %bitcast.3, ...), custom_call_target="tpu_custom_call" | custom-call | tf_op jit(solution)/shard_map/exchange/pallas_call | solution.py:558
  30.1 0.0 copy-done
  30.1 2.3 %finish.1 = bf16[6,1440,256]{2,1,0:T(8,128)(2,1)} custom-call(bf16[6,1440,256]{2,1,0:T(8,128)(2,1)S(1)} %get-tuple-element.9.part_ref, f32[2,384,256]{2,1,0:T(8,128)S(1)} %get-tuple-element.10.early_ref, bf16[2,128,256]{2,1,0:T(8,128)(2,1)S(1)} %get-tuple-element.11.block_ref, bf16[384,128]{1,0:T(8,128)(2,1)S(1)} %get-tuple-element.12.place_ref, ...), custom_call_target="tpu_custom_call" | custom-call | tf_op jit(solution)/shard_map/finish/pallas_call | solution.py:620
Async XLA Ops:
  0.0 30.1 %copy-start = (bf16[1440,192]{1,0:T(8,128)(2,1)S(1)}, bf16[1440,192]{1,0:T(8,128)(2,1)}, u32[]{:S(2)}) copy-start(bf16[1440,192]{1,0:T(8,128)(2,1)} %constant.6.clone.back_table_hbm.back_table_ref) | copy-start | bytes 1658884

commit v4 on v3

--- a/solution.py
+++ b/solution.py
@@ -199,7 +199,6 @@
             pairs = pl.ds(1, lat_pairs - 1)
             each_far(lambda to: copy_to(to, send.at[final, to, pairs], recv.at[i, me, pairs], fwd_sems.at[final]))
 
-        to_near(lambda there: send.at[final, side * near + there], recv.at[i, me], fwd_sems.at[final])
 
     def start_near(pairs):
         near_recv[0, pl.ds(spot, 1), pairs] = send[relay, pl.ds(me, 1), pairs]
@@ -278,6 +277,7 @@
             pairs = pl.ds(0, 1)
             each_far(lambda to: copy_to(to, send.at[final, to, pairs], recv.at[slot_at[final], me, pairs], fwd_sems.at[final]))
 
+        to_near(lambda there: send.at[final, side * near + there], recv.at[slot_at[final], me], fwd_sems.at[final])
         near_lats = jnp.where(lat_in == lat_out + side * hold, 1.0, 0.0).astype(BF16)
         packed_near = dot(packed, near_lats).astype(BF16)
         twice = jnp.where(
@@ -461,18 +461,6 @@
     for p in range(1, lat_pairs):
         start_back(final, pl.ds(p, 1), last_sems.at[p])
 
-    wait_bytes(stat_recv.at[pl.ds(0, near - 1)], stat_sems.at[0, 0])
-    wait_bytes(sum_recv, stat_sems.at[1, 0])
-    wait_bytes(gap_recv, stat_sems.at[2, 0])
-    for k in direct:
-        wait_bytes(recv.at[slot_at[k], pl.ds(0, others)], fwd_sems.at[k, 0])
-    if relay is not None:
-        wait_bytes(near_recv.at[:, pl.ds(0, near - 1)], fwd_sems.at[relay, 0])
-        wait_bytes(pack_recv, pack_sems.at[0])
-        wait_bytes(part_recv, part_sems.at[0])
-        wait_bytes(mixed_recv, mixed_sems.at[0])
-        for which in range(2):
-            wait_bytes(ret.at[relay, pl.ds(0, near - 1)], near_sems.at[which, 0])
     begun = False
     for k in direct[:-1] + ([relay] if relay is not None else []):
         spot_of = place_of(k)
@@ -502,6 +490,19 @@
             filtered = dot(back_table[...], placed[parity * half : (parity + 1) * half])
             field_v[a] = (field_v[a].astype(F32) + filtered).astype(BF16)
 
+    wait_bytes(stat_recv.at[pl.ds(0, near - 1)], stat_sems.at[0, 0])
+    wait_bytes(sum_recv, stat_sems.at[1, 0])
+    wait_bytes(gap_recv, stat_sems.at[2, 0])
+    for k in direct:
+        wait_bytes(recv.at[slot_at[k], pl.ds(0, others)], fwd_sems.at[k, 0])
+    if relay is not None:
+        wait_bytes(near_recv.at[:, pl.ds(0, near - 1)], fwd_sems.at[relay, 0])
+        wait_bytes(pack_recv, pack_sems.at[0])
+        wait_bytes(part_recv, part_sems.at[0])
+        wait_bytes(mixed_recv, mixed_sems.at[0])
+        for which in range(2):
+            wait_bytes(ret.at[relay, pl.ds(0, near - 1)], near_sems.at[which, 0])
+
 
 def finish_kernel(part_ref, early_ref, block_ref, place_ref, back_table_ref, out_hbm, tail, sems):
     lat_dev = part_ref.shape[0]
@@ -547,7 +548,7 @@
     relay = groups - 1 if groups > 1 and 0 < kept_rows < nlat else None
     kept_rows = kept_rows if relay is not None else 8
     high = -(-2 * kept_rows // 8) * 8
-    tall = -(-kept_rows // 16) * 16
+    tall = -(-kept_rows // 8) * 8
     straight = groups - (relay is not None)
     tails = min(2, lat_pairs)
     vmem = pl.BlockSpec(memory_space=pltpu.VMEM)

time: 32.6 us -> 32.5 us (level)
  no operation moved by 1% of the time
where the time goes in v4:
time: 32.5 us; the launch traced here: 32.3 us
  Pallas kernels  32.3 us (99%)
    pallas_call x1, Pallas kernels, per_device(): pl.pallas_call(functools.partial(exchange_kernel, count, pad, relay, kept...  29.9 us
    pallas_call x1, Pallas kernels, per_device(): pl.pallas_call(finish_kernel, out_shape=jax.ShapeDtypeStruct(field.shape,...  2.34 us

profile of v4, /device:TPU:0, one launch (start us, length us, event | category | flops | bytes accessed | tf_op | source)
XLA Modules:
  0.0 32.3 jit_solution(2012975297403029544)
XLA Ops:
  0.0 0.0 copy-start
  0.0 29.9 %exchange.1 = (bf16[6,1440,256]{2,1,0:T(8,128)(2,1)S(1)}, f32[2,384,256]{2,1,0:T(8,128)S(1)}, bf16[2,128,256]{2,1,0:T(8,128)(2,1)S(1)}, bf16[384,128]{1,0:T(8,128)(2,1)S(1)}) custom-call(bf16[6,1440,256]{2,1,0:T(8,128)(2,1)} %field_ref.1, s32[96]{0:T(128)} %wave_hbm.1, s32[1,96]{1,0:T(1,128)} %bitcast.2, f32[1,256]{1,0:T(1,128)} %bitcast.3, ...), custom_call_target="tpu_custom_call" | custom-call | tf_op jit(solution)/shard_map/exchange/pallas_call | solution.py:559
  30.0 0.0 copy-done
  30.0 2.3 %finish.1 = bf16[6,1440,256]{2,1,0:T(8,128)(2,1)} custom-call(bf16[6,1440,256]{2,1,0:T(8,128)(2,1)S(1)} %get-tuple-element.9.part_ref, f32[2,384,256]{2,1,0:T(8,128)S(1)} %get-tuple-element.10.early_ref, bf16[2,128,256]{2,1,0:T(8,128)(2,1)S(1)} %get-tuple-element.11.block_ref, bf16[384,128]{1,0:T(8,128)(2,1)S(1)} %get-tuple-element.12.place_ref, ...), custom_call_target="tpu_custom_call" | custom-call | tf_op jit(solution)/shard_map/finish/pallas_call | solution.py:621
Async XLA Ops:
  0.0 30.0 %copy-start = (bf16[1440,192]{1,0:T(8,128)(2,1)S(1)}, bf16[1440,192]{1,0:T(8,128)(2,1)}, u32[]{:S(2)}) copy-start(bf16[1440,192]{1,0:T(8,128)(2,1)} %constant.6.clone.back_table_hbm.back_table_ref) | copy-start | bytes 1658884
